TPU v7x, 32 devices: a whole 2x2x4 slice. The times are simulated.
32 devices in a mesh: seq: 8 (over y, x, core), head: 4 (over z).
Axes of the slice: x: 2, y: 2, z: 4, core: 2. Of those that a mesh axis runs over, the one named last changes fastest.
Arguments:
- queries: bfloat16 [8192, 2048], P('seq', 'head'), may hold values from -6 to 6
- keys: bfloat16 [8192, 2048], P('seq', 'head'), may hold values from -100 to 100
- values: bfloat16 [8192, 2048], P('seq', 'head'), may hold values from -16 to 16
- gates: float32 [8192, 16], P('seq', 'head'), may hold values from 0.05 to 1
- ridge: float32 [16], P('head'), may hold values from 0.25 to 4
- out_weight: bfloat16 [2048, 2048], P(None, 'head'), may hold values from -0.125 to 0.125
Outputs:
- partial_out: bfloat16 [4, 8192, 2048], P('head', 'seq')
All inputs are finite; a program needn't handle non-finite values.
Results may differ from a plain program's by a relative error of at most 0.0049.
Values may be sent and summed in bfloat16 or wider, within the bound.
A program may use at most 128 MiB of HBM per device.

v0:
```python
import functools

import jax
import jax.numpy as jnp
from jax import lax
from jax.experimental import pallas as pl
from jax.experimental.pallas import tpu as pltpu
from jax.sharding import PartitionSpec as P

HD = 128
SPAN = 128
ITERS = 8
EPS = 1e-06
f32 = jnp.float32
bf16 = jnp.bfloat16
VMEM_BYTES = 56 * 1024 * 1024


def dot(a, b):
    return jnp.dot(a, b, preferred_element_type=f32)


def two_terms(x):
    high = x.astype(bf16)
    return high, (x - high.astype(f32)).astype(bf16)


def inverse_norm(columns):
    return lax.rsqrt(jnp.sum(columns * columns, 0, keepdims=True) + EPS)


def block_sums(keys, values, gate):
    keys_t = keys.astype(f32).T
    s = inverse_norm(keys_t)
    w_value = gate * s
    w_key = w_value * s
    gram = dot(
        jnp.concatenate(two_terms(keys_t * w_key), 1), jnp.concatenate([keys, keys], 0)
    )
    moment = dot(
        jnp.concatenate(two_terms(keys_t * w_value), 1), jnp.concatenate([values, values], 0)
    )
    return gram, moment, keys_t, w_key, w_value


def gate_row(g_ref, h, rows):
    gates = g_ref[:, rows]
    return jnp.sum(
        jnp.where(lax.broadcasted_iota(jnp.int32, gates.shape, 0) == h, gates, 0.0), 0, keepdims=True
    )


def prefix_kernel(
    n_seq, k_ref, v_ref, g_ref, out_ref,
    own, mate, chip_sum, slots, give, final, mate_sems, send_sems, recv_sems, final_sems,
):
    heads = out_ref.shape[0]
    half = heads // 2
    pairs = n_seq // 2
    me = lax.axis_index("seq")
    side = lax.rem(me, 2)
    pair = me // 2
    mate_at = {"seq": me + 1 - 2 * side}
    mine = side * half
    others = (1 - side) * half

    barrier = pltpu.get_barrier_semaphore()
    pl.semaphore_signal(barrier, inc=1, device_id=mate_at, device_id_type=pl.DeviceIdType.MESH)
    for off in range(1, pairs):
        target = {"seq": lax.rem(pair + off, pairs) * 2 + side}
        pl.semaphore_signal(barrier, inc=1, device_id=target, device_id_type=pl.DeviceIdType.MESH)

    def sum_head(h):
        gram = jnp.zeros((HD, HD), f32)
        moment = jnp.zeros((HD, HD), f32)
        columns = pl.ds(pl.multiple_of(h * HD, HD), HD)
        for c in range(k_ref.shape[0] // SPAN):
            rows = pl.ds(c * SPAN, SPAN)
            block_gram, block_moment, *_ = block_sums(
                k_ref[rows, columns], v_ref[rows, columns], gate_row(g_ref, h, rows)
            )
            gram += block_gram
            moment += block_moment
        own[h, 0] = gram
        own[h, 1] = moment

    for j in range(half):
        sum_head(others + j)
    pl.semaphore_wait(barrier, pairs)
    to_mate = pltpu.make_async_remote_copy(
        src_ref=own.at[pl.ds(others, half)], dst_ref=mate,
        send_sem=mate_sems.at[0], recv_sem=mate_sems.at[1],
        device_id=mate_at, device_id_type=pl.DeviceIdType.MESH,
    )
    to_mate.start()
    for j in range(half):
        sum_head(mine + j)
    to_mate.wait()
    chip_sum[...] = own[pl.ds(mine, half)] + mate[...]

    def to_later(off):
        target = {"seq": lax.rem(pair + off, pairs) * 2 + side}
        return pltpu.make_async_remote_copy(
            src_ref=chip_sum, dst_ref=slots.at[off - 1],
            send_sem=send_sems.at[off - 1], recv_sem=recv_sems.at[off - 1],
            device_id=target, device_id_type=pl.DeviceIdType.MESH,
        )

    for off in range(1, pairs):
        @pl.when(pair + off < pairs)
        def _():
            to_later(off).start()

    give[...] = jnp.zeros(give.shape, f32)
    for off in range(1, pairs):
        @pl.when(pair >= off)
        def _():
            to_later(off).wait_recv()
            give[...] = give[...] + slots[off - 1]

    out_ref[pl.ds(mine, half)] = give[...] + side.astype(f32) * mate[...]
    give[...] = give[...] + (1 - side).astype(f32) * own[pl.ds(mine, half)]
    back = pltpu.make_async_remote_copy(
        src_ref=give, dst_ref=final,
        send_sem=final_sems.at[0], recv_sem=final_sems.at[1],
        device_id=mate_at, device_id_type=pl.DeviceIdType.MESH,
    )
    back.start()
    back.wait()
    out_ref[pl.ds(others, half)] = final[...]
    for off in range(1, pairs):
        @pl.when(pair + off < pairs)
        def _():
            to_later(off).wait_send()


def solve_kernel(
    q_ref, k_ref, v_ref, g_ref, ridge_ref, prior_ref, out_ref,
    first, second, weights, weights_value, moments, sol, res, direct,
    terms, corrs, images,
):
    h = pl.program_id(0)
    blocks = k_ref.shape[0] // SPAN
    row = lax.broadcasted_iota(jnp.int32, (HD, HD), 0)
    col = lax.broadcasted_iota(jnp.int32, (HD, HD), 1)
    causal = row <= col
    gram = jnp.where(row == col, ridge_ref[h], 0.0) + prior_ref[0]
    moment = prior_ref[1]
    start = []
    for c in range(blocks):
        rows = pl.ds(c * SPAN, SPAN)
        block_gram, block_moment, keys_t, w_key, w_value = block_sums(
            k_ref[rows], v_ref[rows], gate_row(g_ref, h, rows)
        )
        high, low = two_terms(gram)
        keys = k_ref[rows]
        first[c] = jnp.concatenate([keys, keys], 1)
        second[c] = jnp.concatenate([high, high, low, keys_t.astype(bf16)], 1)
        weights[c] = jnp.where(causal, jnp.broadcast_to(w_key, (SPAN, SPAN)).T, 0.0)
        weights_value[c] = jnp.where(causal, jnp.broadcast_to(w_value, (SPAN, SPAN)).T, 0.0)
        high, low = two_terms(moment)
        moments[c] = jnp.concatenate([high, high, low], 0)
        gram += block_gram
        moment += block_moment
        queries = q_ref[rows].astype(f32).T
        queries = queries * inverse_norm(queries)
        sol[c] = jnp.zeros((HD, SPAN), f32)
        res[c] = queries
        direct[c] = queries
        start.append(jnp.sum(queries * queries, 0, keepdims=True))

    def sweep(_, norms):
        after = []
        for c in range(blocks):
            high, low = two_terms(direct[c])
            terms[c, :HD] = high
            terms[c, HD:] = low
        for c in range(blocks):
            corr = dot(first[c], terms[c])
            corrs[c] = (corr * weights[c]).astype(bf16)
        for c in range(blocks):
            both = terms[c]
            images[c] = dot(second[c], jnp.concatenate([both, both[:HD], corrs[c]], 0))
        for c in range(blocks):
            d = direct[c]
            image = images[c]
            now = norms[c]
            step = now / (jnp.sum(d * image, 0, keepdims=True) + EPS)
            sol[c] = sol[c] + step * d
            r = res[c] - step * image
            res[c] = r
            following = jnp.sum(r * r, 0, keepdims=True)
            direct[c] = r + following / (now + EPS) * d
            after.append(following)
        return tuple(after)

    lax.fori_loop(0, ITERS, sweep, tuple(start))
    for c in range(blocks):
        rows = pl.ds(c * SPAN, SPAN)
        keys = k_ref[rows]
        values = v_ref[rows]
        high, low = two_terms(sol[c])
        corr = dot(jnp.concatenate([keys, keys], 1), jnp.concatenate([high, low], 0))
        corr_high, corr_low = two_terms(corr * weights_value[c])
        left = jnp.concatenate([high, low, high, corr_high, corr_low], 0)
        right = jnp.concatenate([moments[c], values, values], 0)
        out_ref[rows] = lax.dot_general(
            left, right, (((0,), (0,)), ((), ())), preferred_element_type=f32
        ).astype(out_ref.dtype)


def project_kernel(r_ref, *refs):
    *pieces, out_ref = refs
    count = len(pieces)
    me = lax.axis_index("head")
    readout = r_ref[...]
    for shift, piece in enumerate(pieces):
        width = piece.shape[1]
        owner = lax.rem(me + count - shift, count)
        columns = pl.ds(pl.multiple_of(owner * width, width), width)
        out_ref[0, :, columns] = dot(readout, piece[...]).astype(out_ref.dtype)


def shards(n_seq, n_head, queries, keys, values, gates, ridge, out_weight):
    tokens, head_width = queries.shape
    heads = head_width // HD
    blocks = tokens // SPAN
    me = lax.axis_index("head")

    def rows_of(device):
        return lax.dynamic_slice_in_dim(out_weight, device * head_width, head_width, 0)

    pieces = [rows_of(me)]
    for shift in range(1, n_head):
        pairs = [(i, (i + shift) % n_head) for i in range(n_head)]
        pieces.append(lax.ppermute(rows_of(lax.rem(me + shift, n_head)), "head", pairs))

    gate_rows = gates.T
    by_head = pl.BlockSpec((tokens, HD), lambda h: (0, h))
    gate_spec = pl.BlockSpec((heads, tokens), lambda h: (0, 0))
    params = pltpu.CompilerParams(vmem_limit_bytes=VMEM_BYTES)
    tile = SPAN * HD * HD * 2
    half = heads // 2
    pairs = n_seq // 2
    part = pltpu.VMEM((half, 2, HD, HD), f32)
    in_vmem = pl.BlockSpec(memory_space=pltpu.VMEM)
    prior = pl.pallas_call(
        functools.partial(prefix_kernel, n_seq),
        in_specs=[in_vmem] * 3,
        out_specs=in_vmem,
        out_shape=jax.ShapeDtypeStruct((heads, 2, HD, HD), f32),
        scratch_shapes=[
            pltpu.VMEM((heads, 2, HD, HD), f32),
            part, part,
            pltpu.VMEM((pairs - 1, half, 2, HD, HD), f32),
            part, part,
            pltpu.SemaphoreType.DMA((2,)),
            pltpu.SemaphoreType.DMA((pairs - 1,)),
            pltpu.SemaphoreType.DMA((pairs - 1,)),
            pltpu.SemaphoreType.DMA((2,)),
        ],
        compiler_params=pltpu.CompilerParams(
            vmem_limit_bytes=VMEM_BYTES, collective_id=0, has_side_effects=True
        ),
        cost_estimate=pl.CostEstimate(
            flops=heads * blocks * 4 * tile, bytes_accessed=tokens * head_width * 4, transcendentals=0
        ),
        name="prefix",
    )(keys, values, gate_rows)
    state = pltpu.VMEM((blocks, HD, SPAN), f32)
    readout = pl.pallas_call(
        solve_kernel,
        grid=(heads,),
        in_specs=[
            by_head, by_head, by_head, gate_spec,
            pl.BlockSpec(memory_space=pltpu.SMEM),
            pl.BlockSpec((None, 2, HD, HD), lambda h: (h, 0, 0, 0)),
        ],
        out_specs=by_head,
        out_shape=jax.ShapeDtypeStruct((tokens, head_width), bf16),
        scratch_shapes=[
            pltpu.VMEM((blocks, HD, 2 * HD), bf16),
            pltpu.VMEM((blocks, HD, 4 * HD), bf16),
            state, state,
            pltpu.VMEM((blocks, 3 * HD, HD), bf16),
            state, state, state,
            pltpu.VMEM((blocks, 2 * HD, SPAN), bf16),
            pltpu.VMEM((blocks, HD, SPAN), bf16),
            state,
        ],
        compiler_params=params,
        cost_estimate=pl.CostEstimate(
            flops=heads * blocks * 54 * tile, bytes_accessed=tokens * head_width * 8, transcendentals=0
        ),
        name="solve",
    )(queries, keys, values, gate_rows, ridge, prior)
    width = out_weight.shape[1]
    rows = 2 * SPAN
    whole = pl.BlockSpec((head_width, width), lambda i: (0, 0))
    return pl.pallas_call(
        project_kernel,
        grid=(tokens // rows,),
        in_specs=[pl.BlockSpec((rows, head_width), lambda i: (i, 0))] + [whole] * n_head,
        out_specs=pl.BlockSpec((1, rows, width * n_head), lambda i: (0, i, 0)),
        out_shape=jax.ShapeDtypeStruct((1, tokens, width * n_head), bf16),
        compiler_params=params,
        cost_estimate=pl.CostEstimate(
            flops=2 * tokens * head_width * width * n_head,
            bytes_accessed=tokens * width * n_head * 2,
            transcendentals=0,
        ),
        name="project",
    )(readout, *pieces)


def solution(mesh):
    return jax.shard_map(
        functools.partial(shards, mesh.shape["seq"], mesh.shape["head"]),
        mesh=mesh,
        in_specs=(
            P("seq", "head"),
            P("seq", "head"),
            P("seq", "head"),
            P("seq", "head"),
            P("head"),
            P(None, "head"),
        ),
        out_specs=P("head", "seq", None),
        check_vma=False,
    )
```

profile of v0, /device:TPU:13, one launch (start us, length us, event | category | flops | bytes accessed | tf_op | source)
XLA Modules:
  0.0 74.2 jit_solution(967963000142451429)
XLA Ops:
  0.0 2.5 %constant_dynamic-slice_fusion = (bf16[512,512]{1,0:T(8,128)(2,1)S(1)}, bf16[512,512]{1,0:T(8,128)(2,1)S(1)}, bf16[512,512]{1,0:T(8,128)(2,1)}, bf16[512,512]{1,0:T(8,128)(2,1)S(1)}) fusion(bf16[2048,512]{1,0:T(8,128)(2,1)} %param.11, s32[]{:T(128)S(6)} %select_n.15, s32[]{:T(128)S(6)} %select_n.13, s32[]{:T(128)S(6)} %select_n.12, s32[]{:T(128)S(6)} %select_n.14), kind=kLoop, calls=%fused_computation | loop fusion | bytes 4194320 | tf_op jit(solution)/shard_map/dynamic_slice | solution.py:231
  2.5 0.2 collective-permute-start.2
  2.6 1.3 %collective-permute-start = (bf16[512,512]{1,0:T(8,128)(2,1)S(1)}, bf16[512,512]{1,0:T(8,128)(2,1)S(1)}, u32[]{:S(2)}, u32[]{:S(2)}) collective-permute-start(bf16[512,512]{1,0:T(8,128)(2,1)S(1)} %get-tuple-element.6), channel_id=1, source_target_pairs={{0,1},{1,2},{2,3},{3,0},{4,5},{5,6},{6,7},{7,4},{8,9},{9,10},{10,1... | collective-permute-start | bytes 1572872 | tf_op jit(solution)/shard_map/ppermute | solution.py:236
  3.9 4.1 %collective-permute-start.1 = (bf16[512,512]{1,0:T(8,128)(2,1)S(1)}, bf16[512,512]{1,0:T(8,128)(2,1)S(1)}, u32[]{:S(2)}, u32[]{:S(2)}) collective-permute-start(bf16[512,512]{1,0:T(8,128)(2,1)S(1)} %get-tuple-element.8), channel_id=1, source_target_pairs={{0,2},{1,3},{2,0},{3,1},{4,6},{5,7},{6,4},{7,5},{8,10},{9,11},{10,... | collective-permute-start | bytes 1572872 | tf_op jit(solution)/shard_map/ppermute | solution.py:236
  8.0 21.7 %prefix.1.prior_ref = f32[4,2,128,128]{3,2,1,0:T(8,128)} custom-call(bf16[1024,512]{1,0:T(8,128)(2,1)} %k_ref.3, bf16[1024,512]{1,0:T(8,128)(2,1)} %v_ref.3, f32[4,1024]{1,0:T(4,128)} %bitcast.1), custom_call_target="tpu_custom_call" | custom-call | flops 536870912 | bytes 2097152 | tf_op jit(solution)/shard_map/prefix/pallas_call | solution.py:247
  29.7 37.3 %solve.1.r_ref = bf16[1024,512]{1,0:T(8,128)(2,1)} custom-call(bf16[1024,512]{1,0:T(8,128)(2,1)} %q_ref.1, bf16[1024,512]{1,0:T(8,128)(2,1)} %k_ref.3, bf16[1024,512]{1,0:T(8,128)(2,1)} %v_ref.3, f32[4,1024]{1,0:T(4,128)} %bitcast.2, f32[4]{0:T(128)} %ridge_ref.1, f32[4,2,128,128]{3,2,1,0:T(8,128)} %prefix.1.prior_ref), custom_call_target="tpu_custom_call" | custom-call | flops 7247757312 | bytes 4194304 | tf_op jit(solution)/shard_map/solve/pallas_call | solution.py:271
  67.0 0.0 collective-permute-done.2.refs_3_
  67.0 0.0 copy-start
  67.0 0.0 collective-permute-done.refs_1_
  67.0 0.0 copy-start.1
  67.0 0.0 collective-permute-done.1.refs_2_
  67.0 0.0 copy-start.2
  67.0 0.8 %copy-done = bf16[512,512]{1,0:T(8,128)(2,1)} copy-done((bf16[512,512]{1,0:T(8,128)(2,1)}, bf16[512,512]{1,0:T(8,128)(2,1)S(1)}, u32[]{:S(2)}) %copy-start) | copy-done | bytes 524312
  67.8 0.2 copy-done.1
  68.0 0.2 copy-done.2
  68.1 6.1 %project.1 = bf16[1,1024,2048]{2,1,0:T(8,128)(2,1)} custom-call(bf16[1024,512]{1,0:T(8,128)(2,1)} %solve.1.r_ref, bf16[512,512]{1,0:T(8,128)(2,1)} %get-tuple-element.7.refs_0_, bf16[512,512]{1,0:T(8,128)(2,1)} %copy-done.1, bf16[512,512]{1,0:T(8,128)(2,1)} %copy-done.2, bf16[512,512]{1,0:T(8,128)(2,1)} %copy-done), custom_call_target="tpu_custom_call" | custom-call | flops 2147483648 | bytes 4194304 | tf_op jit(solution)/shard_map/project/pallas_call | solution.py:300
Async XLA Ops:
  2.5 64.5 %collective-permute-start.2 = (bf16[512,512]{1,0:T(8,128)(2,1)S(1)}, bf16[512,512]{1,0:T(8,128)(2,1)S(1)}, u32[]{:S(2)}, u32[]{:S(2)}) collective-permute-start(bf16[512,512]{1,0:T(8,128)(2,1)S(1)} %get-tuple-element.5), channel_id=1, source_target_pairs={{0,3},{1,0},{2,1},{3,2},{4,7},{5,4},{6,5},{7,6},{8,11},{9,8},{10,9... | collective-permute-start | bytes 1572872 | tf_op jit(solution)/shard_map/ppermute | solution.py:236
  2.6 64.4 %collective-permute-start = (bf16[512,512]{1,0:T(8,128)(2,1)S(1)}, bf16[512,512]{1,0:T(8,128)(2,1)S(1)}, u32[]{:S(2)}, u32[]{:S(2)}) collective-permute-start(bf16[512,512]{1,0:T(8,128)(2,1)S(1)} %get-tuple-element.6), channel_id=1, source_target_pairs={{0,1},{1,2},{2,3},{3,0},{4,5},{5,6},{6,7},{7,4},{8,9},{9,10},{10,1... | collective-permute-start | bytes 1572872 | tf_op jit(solution)/shard_map/ppermute | solution.py:236
  3.9 63.1 %collective-permute-start.1 = (bf16[512,512]{1,0:T(8,128)(2,1)S(1)}, bf16[512,512]{1,0:T(8,128)(2,1)S(1)}, u32[]{:S(2)}, u32[]{:S(2)}) collective-permute-start(bf16[512,512]{1,0:T(8,128)(2,1)S(1)} %get-tuple-element.8), channel_id=1, source_target_pairs={{0,2},{1,3},{2,0},{3,1},{4,6},{5,7},{6,4},{7,5},{8,10},{9,11},{10,... | collective-permute-start | bytes 1572872 | tf_op jit(solution)/shard_map/ppermute | solution.py:236
  67.0 0.8 %copy-start = (bf16[512,512]{1,0:T(8,128)(2,1)}, bf16[512,512]{1,0:T(8,128)(2,1)S(1)}, u32[]{:S(2)}) copy-start(bf16[512,512]{1,0:T(8,128)(2,1)S(1)} %collective-permute-done.2.refs_3_) | copy-start | bytes 1572868
  67.0 1.0 %copy-start.1 = (bf16[512,512]{1,0:T(8,128)(2,1)}, bf16[512,512]{1,0:T(8,128)(2,1)S(1)}, u32[]{:S(2)}) copy-start(bf16[512,512]{1,0:T(8,128)(2,1)S(1)} %collective-permute-done.refs_1_) | copy-start | bytes 1572868
  67.0 1.1 %copy-start.2 = (bf16[512,512]{1,0:T(8,128)(2,1)}, bf16[512,512]{1,0:T(8,128)(2,1)S(1)}, u32[]{:S(2)}) copy-start(bf16[512,512]{1,0:T(8,128)(2,1)S(1)} %collective-permute-done.1.refs_2_) | copy-start | bytes 1572868
where the time goes:
time: 74.5 us; the launch traced here: 74.2 us
  Pallas kernels  65 us (87%)
  starting transfers between devices  5.57 us (7%)
  local copies, waits for them, and re-layouts  3.55 us (5%)
    pallas_call x1, Pallas kernels, shards(): pl.pallas_call(solve_kernel, grid=(heads,), in_specs=[by_head, by_head, b...  37.3 us
    pallas_call x1, Pallas kernels, shards(): pl.pallas_call(functools.partial(prefix_kernel, n_seq), in_specs=[in_vmem...  21.7 us
    pallas_call x1, Pallas kernels, shards(): pl.pallas_call(project_kernel, grid=(tokens // rows,), in_specs=[pl.Block...  6.08 us
    ppermute x3, starting transfers between devices, shards(): lax.ppermute(rows_of(lax.rem(me + shift, n_head)), 'head', pairs)  5.57 us
    dynamic_slice x1, local copies, waits for them, and re-layouts, rows_of(): lax.dynamic_slice_in_dim(out_weight, device * head_width, head_width, 0)  2.45 us
  transfers between devices with their start and end apart: 3, of which 0 were waited for; matrix products, arithmetic and copies ran while one was open for 0% of the time, Pallas kernels for 79%

commit v1 on v0

--- a/solution.py
+++ b/solution.py
@@ -134,78 +134,74 @@
             to_later(off).wait_send()
 
 
+def row_sum(x):
+    return jnp.sum(x, 1, keepdims=True)
+
+
 def solve_kernel(
     q_ref, k_ref, v_ref, g_ref, ridge_ref, prior_ref, out_ref,
-    first, second, weights, weights_value, moments, sol, res, direct,
-    terms, corrs, images,
+    gram_high, gram_low, keys_t, keys_w, values_w, moment_high, moment_low, sol, res, direct, norms,
 ):
     h = pl.program_id(0)
     blocks = k_ref.shape[0] // SPAN
     row = lax.broadcasted_iota(jnp.int32, (HD, HD), 0)
     col = lax.broadcasted_iota(jnp.int32, (HD, HD), 1)
-    causal = row <= col
-    gram = jnp.where(row == col, ridge_ref[h], 0.0) + prior_ref[0]
-    moment = prior_ref[1]
-    start = []
+    causal = (col <= row).astype(f32).astype(bf16)
+    total = jnp.concatenate([jnp.where(row == col, ridge_ref[h], 0.0) + prior_ref[0], prior_ref[1]], 1)
     for c in range(blocks):
         rows = pl.ds(c * SPAN, SPAN)
-        block_gram, block_moment, keys_t, w_key, w_value = block_sums(
-            k_ref[rows], v_ref[rows], gate_row(g_ref, h, rows)
-        )
-        high, low = two_terms(gram)
         keys = k_ref[rows]
-        first[c] = jnp.concatenate([keys, keys], 1)
-        second[c] = jnp.concatenate([high, high, low, keys_t.astype(bf16)], 1)
-        weights[c] = jnp.where(causal, jnp.broadcast_to(w_key, (SPAN, SPAN)).T, 0.0)
-        weights_value[c] = jnp.where(causal, jnp.broadcast_to(w_value, (SPAN, SPAN)).T, 0.0)
-        high, low = two_terms(moment)
-        moments[c] = jnp.concatenate([high, high, low], 0)
-        gram += block_gram
-        moment += block_moment
-        queries = q_ref[rows].astype(f32).T
-        queries = queries * inverse_norm(queries)
-        sol[c] = jnp.zeros((HD, SPAN), f32)
+        keys_f = keys.astype(f32)
+        s = lax.rsqrt(row_sum(keys_f * keys_f) + EPS)
+        gates = g_ref[rows, :]
+        gate = row_sum(jnp.where(lax.broadcasted_iota(jnp.int32, gates.shape, 1) == h, gates, 0.0))
+        w_value = gate * s
+        both = jnp.concatenate([keys_f * (w_value * s), v_ref[rows].astype(f32) * w_value], 1)
+        high, low = two_terms(both)
+        turned = keys.T
+        keys_t[c] = turned
+        keys_w[c] = high[:, :HD]
+        values_w[c] = high[:, HD:]
+        total_high, total_low = two_terms(total)
+        gram_high[c] = total_high[:, :HD]
+        gram_low[c] = total_low[:, :HD]
+        moment_high[c] = total_high[:, HD:]
+        moment_low[c] = total_low[:, HD:]
+        total += dot(jnp.concatenate([turned, turned], 1), jnp.concatenate([high, low], 0))
+        queries = q_ref[rows].astype(f32)
+        queries = queries * lax.rsqrt(row_sum(queries * queries) + EPS)
         res[c] = queries
         direct[c] = queries
-        start.append(jnp.sum(queries * queries, 0, keepdims=True))
-
-    def sweep(_, norms):
-        after = []
-        for c in range(blocks):
-            high, low = two_terms(direct[c])
-            terms[c, :HD] = high
-            terms[c, HD:] = low
-        for c in range(blocks):
-            corr = dot(first[c], terms[c])
-            corrs[c] = (corr * weights[c]).astype(bf16)
-        for c in range(blocks):
-            both = terms[c]
-            images[c] = dot(second[c], jnp.concatenate([both, both[:HD], corrs[c]], 0))
+        sol[c] = jnp.zeros((SPAN, HD), f32)
+        norms[c] = jnp.broadcast_to(row_sum(queries * queries), (SPAN, HD))
+
+    def apply(c, d, high_ref, low_ref, right_ref):
+        high, low = two_terms(d)
+        half = jnp.concatenate([high_ref[c], keys_t[c]], 1)
+        first = dot(jnp.concatenate([high, low], 1), jnp.concatenate([half, half], 0))
+        corr = first[:, HD:].astype(bf16) * causal
+        return first[:, :HD] + dot(
+            jnp.concatenate([corr, high], 1), jnp.concatenate([right_ref[c], low_ref[c]], 0)
+        )
+
+    def sweep(_, carry):
         for c in range(blocks):
             d = direct[c]
-            image = images[c]
+            image = apply(c, d, gram_high, gram_low, keys_w)
             now = norms[c]
-            step = now / (jnp.sum(d * image, 0, keepdims=True) + EPS)
+            step = now / (row_sum(d * image) + EPS)
             sol[c] = sol[c] + step * d
             r = res[c] - step * image
             res[c] = r
-            following = jnp.sum(r * r, 0, keepdims=True)
+            following = jnp.broadcast_to(row_sum(r * r), (SPAN, HD))
+            norms[c] = following
             direct[c] = r + following / (now + EPS) * d
-            after.append(following)
-        return tuple(after)
-
-    lax.fori_loop(0, ITERS, sweep, tuple(start))
+        return carry
+
+    lax.fori_loop(0, ITERS, sweep, 0)
     for c in range(blocks):
-        rows = pl.ds(c * SPAN, SPAN)
-        keys = k_ref[rows]
-        values = v_ref[rows]
-        high, low = two_terms(sol[c])
-        corr = dot(jnp.concatenate([keys, keys], 1), jnp.concatenate([high, low], 0))
-        corr_high, corr_low = two_terms(corr * weights_value[c])
-        left = jnp.concatenate([high, low, high, corr_high, corr_low], 0)
-        right = jnp.concatenate([moments[c], values, values], 0)
-        out_ref[rows] = lax.dot_general(
-            left, right, (((0,), (0,)), ((), ())), preferred_element_type=f32
+        out_ref[pl.ds(c * SPAN, SPAN)] = apply(
+            c, sol[c], moment_high, moment_low, values_w
         ).astype(out_ref.dtype)
 
 
@@ -268,32 +264,27 @@
         name="prefix",
     )(keys, values, gate_rows)
     state = pltpu.VMEM((blocks, HD, SPAN), f32)
+    tile_bf16 = pltpu.VMEM((blocks, SPAN, HD), bf16)
     readout = pl.pallas_call(
         solve_kernel,
         grid=(heads,),
         in_specs=[
-            by_head, by_head, by_head, gate_spec,
+            by_head, by_head, by_head, pl.BlockSpec((tokens, heads), lambda h: (0, 0)),
             pl.BlockSpec(memory_space=pltpu.SMEM),
             pl.BlockSpec((None, 2, HD, HD), lambda h: (h, 0, 0, 0)),
         ],
         out_specs=by_head,
         out_shape=jax.ShapeDtypeStruct((tokens, head_width), bf16),
         scratch_shapes=[
-            pltpu.VMEM((blocks, HD, 2 * HD), bf16),
-            pltpu.VMEM((blocks, HD, 4 * HD), bf16),
-            state, state,
-            pltpu.VMEM((blocks, 3 * HD, HD), bf16),
-            state, state, state,
-            pltpu.VMEM((blocks, 2 * HD, SPAN), bf16),
-            pltpu.VMEM((blocks, HD, SPAN), bf16),
-            state,
+            *[tile_bf16] * 7,
+            state, state, state, state,
         ],
         compiler_params=params,
         cost_estimate=pl.CostEstimate(
             flops=heads * blocks * 54 * tile, bytes_accessed=tokens * head_width * 8, transcendentals=0
         ),
         name="solve",
-    )(queries, keys, values, gate_rows, ridge, prior)
+    )(queries, keys, values, gates, ridge, prior)
     width = out_weight.shape[1]
     rows = 2 * SPAN
     whole = pl.BlockSpec((head_width, width), lambda i: (0, 0))

time: 74.5 us -> 75.3 us (1.011)
  local copies, waits for them, and re-layouts: 3.55 us -> 4.66 us
    unnamed x6 -> x9, local copies, waits for them, and re-layouts: 1.1 us -> 2.13 us
  transfers between devices with their start and end apart: 3 -> 3, of which waited for: 0 -> 0; matrix products, arithmetic and copies ran while one was open for 0% -> 1% of each run, Pallas kernels for 79% -> 78%
where the time goes in v1:
time: 75.3 us; the launch traced here: 75 us
  Pallas kernels  64.7 us (86%)
  starting transfers between devices  5.57 us (7%)
  local copies, waits for them, and re-layouts  4.66 us (6%)
    pallas_call x1, Pallas kernels, shards(): pl.pallas_call(solve_kernel, grid=(heads,), in_specs=[by_head, by_head, b...  37 us
    pallas_call x1, Pallas kernels, shards(): pl.pallas_call(functools.partial(prefix_kernel, n_seq), in_specs=[in_vmem...  21.7 us
    pallas_call x1, Pallas kernels, shards(): pl.pallas_call(project_kernel, grid=(tokens // rows,), in_specs=[pl.Block...  6.08 us
    ppermute x3, starting transfers between devices, shards(): lax.ppermute(rows_of(lax.rem(me + shift, n_head)), 'head', pairs)  5.57 us
    dynamic_slice x1, local copies, waits for them, and re-layouts, rows_of(): lax.dynamic_slice_in_dim(out_weight, device * head_width, head_width, 0)  2.53 us
    unnamed x9, local copies, waits for them, and re-layouts  2.13 us
  transfers between devices with their start and end apart: 3, of which 0 were waited for; matrix products, arithmetic and copies ran while one was open for 1% of the time, Pallas kernels for 78%

profile of v1, /device:TPU:13, one launch (start us, length us, event | category | flops | bytes accessed | tf_op | source)
XLA Modules:
  0.0 75.0 jit_solution(9869140581878035363)
XLA Ops:
  0.0 0.0 copy-start
  0.0 2.5 %constant_dynamic-slice_fusion = (bf16[512,512]{1,0:T(8,128)(2,1)S(1)}, bf16[512,512]{1,0:T(8,128)(2,1)S(1)}, bf16[512,512]{1,0:T(8,128)(2,1)}, bf16[512,512]{1,0:T(8,128)(2,1)S(1)}) fusion(bf16[2048,512]{1,0:T(8,128)(2,1)} %param.11, s32[]{:T(128)S(6)} %select_n.15, s32[]{:T(128)S(6)} %select_n.13, s32[]{:T(128)S(6)} %select_n.12, s32[]{:T(128)S(6)} %select_n.14), kind=kLoop, calls=%fused_computation | loop fusion | bytes 4194320 | tf_op jit(solution)/shard_map/dynamic_slice | solution.py:227
  2.5 0.2 collective-permute-start.2
  2.7 1.3 %collective-permute-start = (bf16[512,512]{1,0:T(8,128)(2,1)S(1)}, bf16[512,512]{1,0:T(8,128)(2,1)S(1)}, u32[]{:S(2)}, u32[]{:S(2)}) collective-permute-start(bf16[512,512]{1,0:T(8,128)(2,1)S(1)} %get-tuple-element.6), channel_id=1, source_target_pairs={{0,1},{1,2},{2,3},{3,0},{4,5},{5,6},{6,7},{7,4},{8,9},{9,10},{10,1... | collective-permute-start | bytes 1572872 | tf_op jit(solution)/shard_map/ppermute | solution.py:232
  4.0 4.1 %collective-permute-start.1 = (bf16[512,512]{1,0:T(8,128)(2,1)S(1)}, bf16[512,512]{1,0:T(8,128)(2,1)S(1)}, u32[]{:S(2)}, u32[]{:S(2)}) collective-permute-start(bf16[512,512]{1,0:T(8,128)(2,1)S(1)} %get-tuple-element.8), channel_id=1, source_target_pairs={{0,2},{1,3},{2,0},{3,1},{4,6},{5,7},{6,4},{7,5},{8,10},{9,11},{10,... | collective-permute-start | bytes 1572872 | tf_op jit(solution)/shard_map/ppermute | solution.py:232
  8.1 0.0 copy-done
  8.1 1.0 %copy.7.g_ref = f32[1024,4]{1,0:T(8,128)} copy(f32[1024,4]{0,1:T(4,128)S(1)} %copy-done) | data formatting | bytes 32768 | tf_op args[3]
  9.1 21.7 %prefix.1.prior_ref = f32[4,2,128,128]{3,2,1,0:T(8,128)} custom-call(bf16[1024,512]{1,0:T(8,128)(2,1)} %k_ref.3, bf16[1024,512]{1,0:T(8,128)(2,1)} %v_ref.3, f32[4,1024]{1,0:T(4,128)} %bitcast.1), custom_call_target="tpu_custom_call" | custom-call | flops 536870912 | bytes 2097152 | tf_op jit(solution)/shard_map/prefix/pallas_call | solution.py:243
  30.8 37.0 %solve.1.r_ref = bf16[1024,512]{1,0:T(8,128)(2,1)} custom-call(bf16[1024,512]{1,0:T(8,128)(2,1)} %q_ref.1, bf16[1024,512]{1,0:T(8,128)(2,1)} %k_ref.3, bf16[1024,512]{1,0:T(8,128)(2,1)} %v_ref.3, f32[1024,4]{1,0:T(8,128)} %copy.7.g_ref, f32[4]{0:T(128)} %ridge_ref.1, f32[4,2,128,128]{3,2,1,0:T(8,128)} %prefix.1.prior_ref), custom_call_target="tpu_custom_call" | custom-call | flops 7247757312 | bytes 4194304 | tf_op jit(solution)/shard_map/solve/pallas_call | solution.py:268
  67.8 0.0 collective-permute-done.2.refs_3_
  67.8 0.0 copy-start.1
  67.8 0.0 collective-permute-done.refs_1_
  67.8 0.0 copy-start.2
  67.8 0.0 collective-permute-done.1.refs_2_
  67.8 0.0 copy-start.3
  67.8 0.8 %copy-done.1 = bf16[512,512]{1,0:T(8,128)(2,1)} copy-done((bf16[512,512]{1,0:T(8,128)(2,1)}, bf16[512,512]{1,0:T(8,128)(2,1)S(1)}, u32[]{:S(2)}) %copy-start.1) | copy-done | bytes 524312
  68.6 0.2 copy-done.2
  68.8 0.2 copy-done.3
  68.9 6.1 %project.1 = bf16[1,1024,2048]{2,1,0:T(8,128)(2,1)} custom-call(bf16[1024,512]{1,0:T(8,128)(2,1)} %solve.1.r_ref, bf16[512,512]{1,0:T(8,128)(2,1)} %get-tuple-element.7.refs_0_, bf16[512,512]{1,0:T(8,128)(2,1)} %copy-done.2, bf16[512,512]{1,0:T(8,128)(2,1)} %copy-done.3, bf16[512,512]{1,0:T(8,128)(2,1)} %copy-done.1), custom_call_target="tpu_custom_call" | custom-call | flops 2147483648 | bytes 4194304 | tf_op jit(solution)/shard_map/project/pallas_call | solution.py:291
Async XLA Ops:
  0.0 8.1 %copy-start = (f32[1024,4]{0,1:T(4,128)S(1)}, f32[1024,4]{0,1:T(4,128)}, u32[]{:S(2)}) copy-start(f32[1024,4]{0,1:T(4,128)} %param.9) | copy-start | bytes 49156
  2.5 65.2 %collective-permute-start.2 = (bf16[512,512]{1,0:T(8,128)(2,1)S(1)}, bf16[512,512]{1,0:T(8,128)(2,1)S(1)}, u32[]{:S(2)}, u32[]{:S(2)}) collective-permute-start(bf16[512,512]{1,0:T(8,128)(2,1)S(1)} %get-tuple-element.5), channel_id=1, source_target_pairs={{0,3},{1,0},{2,1},{3,2},{4,7},{5,4},{6,5},{7,6},{8,11},{9,8},{10,9... | collective-permute-start | bytes 1572872 | tf_op jit(solution)/shard_map/ppermute | solution.py:232
  2.7 65.1 %collective-permute-start = (bf16[512,512]{1,0:T(8,128)(2,1)S(1)}, bf16[512,512]{1,0:T(8,128)(2,1)S(1)}, u32[]{:S(2)}, u32[]{:S(2)}) collective-permute-start(bf16[512,512]{1,0:T(8,128)(2,1)S(1)} %get-tuple-element.6), channel_id=1, source_target_pairs={{0,1},{1,2},{2,3},{3,0},{4,5},{5,6},{6,7},{7,4},{8,9},{9,10},{10,1... | collective-permute-start | bytes 1572872 | tf_op jit(solution)/shard_map/ppermute | solution.py:232
  4.0 63.8 %collective-permute-start.1 = (bf16[512,512]{1,0:T(8,128)(2,1)S(1)}, bf16[512,512]{1,0:T(8,128)(2,1)S(1)}, u32[]{:S(2)}, u32[]{:S(2)}) collective-permute-start(bf16[512,512]{1,0:T(8,128)(2,1)S(1)} %get-tuple-element.8), channel_id=1, source_target_pairs={{0,2},{1,3},{2,0},{3,1},{4,6},{5,7},{6,4},{7,5},{8,10},{9,11},{10,... | collective-permute-start | bytes 1572872 | tf_op jit(solution)/shard_map/ppermute | solution.py:232
  67.8 0.8 %copy-start.1 = (bf16[512,512]{1,0:T(8,128)(2,1)}, bf16[512,512]{1,0:T(8,128)(2,1)S(1)}, u32[]{:S(2)}) copy-start(bf16[512,512]{1,0:T(8,128)(2,1)S(1)} %collective-permute-done.2.refs_3_) | copy-start | bytes 1572868
  67.8 1.0 %copy-start.2 = (bf16[512,512]{1,0:T(8,128)(2,1)}, bf16[512,512]{1,0:T(8,128)(2,1)S(1)}, u32[]{:S(2)}) copy-start(bf16[512,512]{1,0:T(8,128)(2,1)S(1)} %collective-permute-done.refs_1_) | copy-start | bytes 1572868
  67.8 1.1 %copy-start.3 = (bf16[512,512]{1,0:T(8,128)(2,1)}, bf16[512,512]{1,0:T(8,128)(2,1)S(1)}, u32[]{:S(2)}) copy-start(bf16[512,512]{1,0:T(8,128)(2,1)S(1)} %collective-permute-done.1.refs_2_) | copy-start | bytes 1572868

commit v2 on v1

v2 whole, which is shorter than its diff:
```python
import functools

import jax
import jax.numpy as jnp
from jax import lax
from jax.experimental import pallas as pl
from jax.experimental.pallas import tpu as pltpu
from jax.sharding import PartitionSpec as P

HD = 128
SPAN = 128
ITERS = 8
EPS = 1e-06
f32 = jnp.float32
bf16 = jnp.bfloat16
VMEM_BYTES = 56 * 1024 * 1024
MESH = pl.DeviceIdType.MESH


def dot(a, b):
    return jnp.dot(a, b, preferred_element_type=f32)


def two_terms(x):
    high = x.astype(bf16)
    return high, (x - high.astype(f32)).astype(bf16)


def row_sum(x):
    return jnp.sum(x, 1, keepdims=True)


def wide(x):
    return jnp.broadcast_to(x, (SPAN, HD))


def solve_kernel(
    n_seq, n_head,
    k_hbm, v_hbm, q_hbm, g_ref, ridge_ref, w_hbm, out_ref, pieces_ref,
    k_ref, v_ref, q_ref, keys_t, keys_w, values_w, scales, gram_local, moment_local,
    gram_high, gram_low, direct, res, sol, norms, images,
    own, mate, chip_sum, slots, give, prior,
    load_sems, piece_sems, mate_sems, send_sems, recv_sems, back_sems,
):
    tokens, head_width = k_ref.shape
    heads = head_width // HD
    half = heads // 2
    blocks = tokens // SPAN
    pairs = n_seq // 2
    me = lax.axis_index("seq")
    group = lax.axis_index("head")
    side = lax.rem(me, 2)
    pair = me // 2
    mate_at = {"seq": me + 1 - 2 * side}
    mine = side * half
    others = (1 - side) * half
    row = lax.broadcasted_iota(jnp.int32, (HD, HD), 0)
    col = lax.broadcasted_iota(jnp.int32, (HD, HD), 1)
    causal = (col <= row).astype(f32).astype(bf16)
    GRAM, MOMENT = 0, 1

    loads = [
        pltpu.make_async_copy(src, dst, load_sems.at[i])
        for i, (src, dst) in enumerate(((k_hbm, k_ref), (v_hbm, v_ref), (q_hbm, q_ref)))
    ]
    for load in loads:
        load.start()

    barrier = pltpu.get_barrier_semaphore()
    pl.semaphore_signal(barrier, inc=1, device_id=mate_at, device_id_type=MESH)
    for off in range(1, pairs):
        target = {"seq": lax.rem(pair + off, pairs) * 2 + side}
        pl.semaphore_signal(barrier, inc=1, device_id=target, device_id_type=MESH)
    for shift in range(1, n_head):
        target = {"head": lax.rem(group + shift, n_head)}
        pl.semaphore_signal(barrier, inc=1, device_id=target, device_id_type=MESH)

    def columns_of(h):
        return pl.ds(pl.multiple_of(h * HD, HD), HD)

    def sum_grams(first):
        def one(j, carry):
            h = first + j
            total = jnp.zeros((HD, HD), f32)
            for c in range(blocks):
                n = h * blocks + c
                rows = pl.ds(c * SPAN, SPAN)
                keys = k_ref[rows, columns_of(h)]
                keys_f = keys.astype(f32)
                s = lax.rsqrt(row_sum(keys_f * keys_f) + EPS)
                gates = g_ref[rows, :]
                gate = row_sum(jnp.where(lax.broadcasted_iota(jnp.int32, gates.shape, 1) == h, gates, 0.0))
                w_value = gate * s
                high, low = two_terms(keys_f * (w_value * s))
                turned = keys.T
                keys_t[n] = turned
                keys_w[n] = high
                scales[n] = wide(w_value)
                gram_local[n] = total
                total += dot(jnp.concatenate([turned, turned], 1), jnp.concatenate([high, low], 0))
            own[GRAM, h] = total
            return carry

        lax.fori_loop(0, half, one, 0)

    def sum_moments(first):
        def one(j, carry):
            h = first + j
            total = jnp.zeros((HD, HD), f32)
            for c in range(blocks):
                n = h * blocks + c
                values = v_ref[pl.ds(c * SPAN, SPAN), columns_of(h)].astype(f32)
                high, low = two_terms(values * scales[n])
                values_w[n] = high
                moment_local[n] = total
                turned = keys_t[n]
                total += dot(jnp.concatenate([turned, turned], 1), jnp.concatenate([high, low], 0))
            own[MOMENT, h] = total
            return carry

        lax.fori_loop(0, half, one, 0)

    def to_mate(kind):
        return pltpu.make_async_remote_copy(
            src_ref=own.at[kind, pl.ds(others, half)], dst_ref=mate.at[kind],
            send_sem=mate_sems.at[kind, 0], recv_sem=mate_sems.at[kind, 1],
            device_id=mate_at, device_id_type=MESH,
        )

    def to_later(kind, off):
        target = {"seq": lax.rem(pair + off, pairs) * 2 + side}
        return pltpu.make_async_remote_copy(
            src_ref=chip_sum.at[kind], dst_ref=slots.at[kind, off - 1],
            send_sem=send_sems.at[kind, off - 1], recv_sem=recv_sems.at[kind, off - 1],
            device_id=target, device_id_type=MESH,
        )

    def to_back(kind):
        return pltpu.make_async_remote_copy(
            src_ref=give.at[kind], dst_ref=prior.at[kind, 1],
            send_sem=back_sems.at[kind, 0], recv_sem=back_sems.at[kind, 1],
            device_id=mate_at, device_id_type=MESH,
        )

    def to_head(shift):
        target = lax.rem(group + shift, n_head)
        return pltpu.make_async_remote_copy(
            src_ref=w_hbm.at[pl.ds(pl.multiple_of(target * head_width, head_width), head_width)],
            dst_ref=pieces_ref.at[shift - 1],
            send_sem=piece_sems.at[0, shift - 1], recv_sem=piece_sems.at[1, shift - 1],
            device_id={"head": target}, device_id_type=MESH,
        )

    def pass_on(kind):
        to_mate(kind).wait_recv()
        chip_sum[kind] = own[kind, pl.ds(mine, half)] + mate[kind]
        for off in range(1, pairs):
            @pl.when(pair + off < pairs)
            def _():
                to_later(kind, off).start()

    def collect(kind):
        total = jnp.zeros((half, HD, HD), f32)
        give[kind] = total
        for off in range(1, pairs):
            @pl.when(pair >= off)
            def _():
                to_later(kind, off).wait_recv()
                give[kind] = give[kind] + slots[kind, off - 1]
        prior[kind, 0] = give[kind] + side.astype(f32) * mate[kind]
        give[kind] = give[kind] + (1 - side).astype(f32) * own[kind, pl.ds(mine, half)]
        to_back(kind).start()

    loads[0].wait()
    sum_grams(others)
    pl.semaphore_wait(barrier, pairs + n_head - 1)
    to_mate(GRAM).start()
    for shift in range(1, n_head):
        to_head(shift).start()
    sum_grams(mine)
    pass_on(GRAM)
    loads[1].wait()
    sum_moments(others)
    to_mate(MOMENT).start()
    sum_moments(mine)
    pass_on(MOMENT)
    loads[2].wait()
    collect(GRAM)

    def apply(n, at, d, high_ref, low_ref, right_ref, fine=True):
        half_right = jnp.concatenate([high_ref[n], keys_t[at]], 1)
        if fine:
            high, low = two_terms(d)
            first = dot(jnp.concatenate([high, low], 1), jnp.concatenate([half_right, half_right], 0))
        else:
            high = d.astype(bf16)
            first = dot(high, half_right)
        corr = first[:, HD:].astype(bf16) * causal
        if fine:
            left = jnp.concatenate([corr, high], 1)
            right = jnp.concatenate([right_ref[at], low_ref[n]], 0)
        else:
            left, right = corr, right_ref[at]
        second = dot(left, jnp.concatenate([right, right], 1))
        return first[:, :HD] + second[:, :HD]

    units = half * blocks
    behind = units // 2

    def run(p, carry):
        first = mine + p * (others - mine)

        @pl.when(p == 1)
        def _():
            to_back(GRAM).wait_recv()

        def split(kind, j, c, local, low_too=None):
            total = local[(first + j) * blocks + c] + prior[kind, p, j]
            if kind == GRAM:
                total += jnp.where(row == col, ridge_ref[first + j], 0.0)
            gram_high[j * blocks + c], gram_low[j * blocks + c] = two_terms(total)

        def prepare(j, carry):
            for c in range(blocks):
                n = j * blocks + c
                split(GRAM, j, c, gram_local)
                queries = q_ref[pl.ds(c * SPAN, SPAN), columns_of(first + j)].astype(f32)
                square = row_sum(queries * queries)
                scale = lax.rsqrt(square + EPS)
                queries = queries * scale
                res[n] = queries
                direct[n] = queries
                sol[n] = jnp.zeros((SPAN, HD), f32)
                norms[n] = wide(square * scale * scale)
            return carry

        lax.fori_loop(0, half, prepare, 0)

        def multiply(n, fine=True):
            images[n] = apply(n, first * blocks + n, direct[n], gram_high, gram_low, keys_w, fine)

        def update(n, last=False):
            d = direct[n]
            image = images[n]
            now = norms[n]
            step = now / (row_sum(d * image) + EPS)
            sol[n] = sol[n] + step * d
            if last:
                return
            r = res[n] - step * image
            res[n] = r
            following = wide(row_sum(r * r))
            norms[n] = following
            direct[n] = r + following / (now + EPS) * d

        def iteration(last=False, before_last=False):
            for n in range(behind):
                multiply(n, not last)
                update(behind + n, last)
            for n in range(behind):
                update(n, last)
                if not last:
                    multiply(behind + n, not before_last)

        for n in range(behind):
            multiply(behind + n)

        def sweep(_, carry):
            iteration()
            iteration()
            return carry

        lax.fori_loop(0, (ITERS - 2) // 2, sweep, 0)
        iteration(before_last=True)
        iteration(last=True)

        @pl.when(p == 0)
        def _():
            collect(MOMENT)

        @pl.when(p == 1)
        def _():
            to_back(MOMENT).wait_recv()

        def finish(j, carry):
            for c in range(blocks):
                split(MOMENT, j, c, moment_local)
            for c in range(blocks):
                n = j * blocks + c
                out_ref[pl.ds(c * SPAN, SPAN), columns_of(first + j)] = apply(
                    n, first * blocks + n, sol[n], gram_high, gram_low, values_w
                ).astype(out_ref.dtype)
            return carry

        lax.fori_loop(0, half, finish, 0)
        return carry

    lax.fori_loop(0, 2, run, 0)
    for kind in (GRAM, MOMENT):
        to_mate(kind).wait_send()
        to_back(kind).wait_send()
        for off in range(1, pairs):
            @pl.when(pair + off < pairs)
            def _():
                to_later(kind, off).wait_send()
    for shift in range(1, n_head):
        to_head(shift).wait()


def project_kernel(r_ref, w_hbm, pieces_ref, out_ref, weight, sems):
    count = pieces_ref.shape[0] + 1
    depth, width = pieces_ref.shape[1:]
    me = lax.axis_index("head")

    @pl.when(pl.program_id(0) == 0)
    def _():
        copies = []
        for shift in range(count):
            owner = lax.rem(me + count - shift, count)
            if shift:
                source = pieces_ref.at[shift - 1]
            else:
                source = w_hbm.at[pl.ds(pl.multiple_of(me * depth, depth), depth)]
            columns = pl.ds(pl.multiple_of(owner * width, width), width)
            copies.append(pltpu.make_async_copy(source, weight.at[:, columns], sems.at[shift]))
        for copy in copies:
            copy.start()
        for copy in copies:
            copy.wait()

    out_ref[0] = dot(r_ref[...], weight[...]).astype(out_ref.dtype)


def shards(n_seq, n_head, queries, keys, values, gates, ridge, out_weight):
    tokens, head_width = queries.shape
    heads = head_width // HD
    half = heads // 2
    blocks = tokens // SPAN
    pairs = n_seq // 2
    width = out_weight.shape[1]
    tile = SPAN * HD * HD * 2
    hbm = pl.BlockSpec(memory_space=pl.ANY)
    in_vmem = pl.BlockSpec(memory_space=pltpu.VMEM)

    def square(*lead, dtype=f32):
        return pltpu.VMEM((*lead, HD, HD), dtype)

    every, some = heads * blocks, half * blocks
    readout, pieces = pl.pallas_call(
        functools.partial(solve_kernel, n_seq, n_head),
        in_specs=[hbm, hbm, hbm, in_vmem, pl.BlockSpec(memory_space=pltpu.SMEM), hbm],
        out_specs=[in_vmem, hbm],
        out_shape=[
            jax.ShapeDtypeStruct((tokens, head_width), bf16),
            jax.ShapeDtypeStruct((n_head - 1, head_width, width), bf16),
        ],
        scratch_shapes=[
            *[pltpu.VMEM((tokens, head_width), bf16)] * 3,
            *[square(every, dtype=bf16)] * 3,
            *[square(every)] * 3,
            *[square(some, dtype=bf16)] * 2,
            *[square(some)] * 5,
            square(2, heads),
            square(2, half), square(2, half), square(2, pairs - 1, half), square(2, half), square(2, 2, half),
            pltpu.SemaphoreType.DMA((3,)),
            pltpu.SemaphoreType.DMA((2, n_head - 1)),
            pltpu.SemaphoreType.DMA((2, 2)),
            pltpu.SemaphoreType.DMA((2, pairs - 1)),
            pltpu.SemaphoreType.DMA((2, pairs - 1)),
            pltpu.SemaphoreType.DMA((2, 2)),
        ],
        compiler_params=pltpu.CompilerParams(
            vmem_limit_bytes=VMEM_BYTES, collective_id=0, has_side_effects=True
        ),
        cost_estimate=pl.CostEstimate(
            flops=heads * blocks * 58 * tile, bytes_accessed=tokens * head_width * 8, transcendentals=0
        ),
        name="solve",
    )(keys, values, queries, gates, ridge, out_weight)
    rows = 2 * SPAN
    return pl.pallas_call(
        project_kernel,
        grid=(tokens // rows,),
        in_specs=[pl.BlockSpec((rows, head_width), lambda i: (i, 0)), hbm, hbm],
        out_specs=pl.BlockSpec((1, rows, width * n_head), lambda i: (0, i, 0)),
        out_shape=jax.ShapeDtypeStruct((1, tokens, width * n_head), bf16),
        scratch_shapes=[
            pltpu.VMEM((head_width, width * n_head), bf16),
            pltpu.SemaphoreType.DMA((n_head,)),
        ],
        compiler_params=pltpu.CompilerParams(vmem_limit_bytes=VMEM_BYTES),
        cost_estimate=pl.CostEstimate(
            flops=2 * tokens * head_width * width * n_head,
            bytes_accessed=tokens * width * n_head * 2,
            transcendentals=0,
        ),
        name="project",
    )(readout, out_weight, pieces)


def solution(mesh):
    return jax.shard_map(
        functools.partial(shards, mesh.shape["seq"], mesh.shape["head"]),
        mesh=mesh,
        in_specs=(
            P("seq", "head"),
            P("seq", "head"),
            P("seq", "head"),
            P("seq", "head"),
            P("head"),
            P(None, "head"),
        ),
        out_specs=P("head", "seq", None),
        check_vma=False,
    )
```

time: 75.3 us -> 61.4 us (0.82)
  the two profiles are of different devices: /device:TPU:13 before, /device:TPU:8 now
where the time goes in v2:
time: 61.4 us; the launch traced here: 61.1 us
  Pallas kernels  59.3 us (97%)
  local copies, waits for them, and re-layouts  1.74 us (3%)
    pallas_call x1, Pallas kernels, shards(): pl.pallas_call(functools.partial(solve_kernel, n_seq, n_head), in_specs=[...  52.3 us
    pallas_call x1, Pallas kernels, shards(): pl.pallas_call(project_kernel, grid=(tokens // rows,), in_specs=[pl.Block...  7.03 us
    unnamed x1, local copies, waits for them, and re-layouts  1.74 us

profile of v2, /device:TPU:8, one launch (start us, length us, event | category | flops | bytes accessed | tf_op | source)
XLA Modules:
  0.0 61.1 jit_solution(10470350421998296809)
XLA Ops:
  0.0 1.7 %copy.7.g_ref = f32[1024,4]{1,0:T(8,128)} copy(f32[1024,4]{0,1:T(4,128)} %param.9) | data formatting | bytes 32768 | tf_op args[3]
  1.7 52.3 %solve.1 = (bf16[1024,512]{1,0:T(8,128)(2,1)}, bf16[3,512,512]{2,1,0:T(8,128)(2,1)}) custom-call(bf16[1024,512]{1,0:T(8,128)(2,1)} %k_hbm.1, bf16[1024,512]{1,0:T(8,128)(2,1)} %v_hbm.1, bf16[1024,512]{1,0:T(8,128)(2,1)} %q_hbm.1, f32[1024,4]{1,0:T(8,128)} %copy.7.g_ref, f32[4]{0:T(128)} %ridge_ref.1, bf16[2048,512]{1,0:T(8,128)(2,1)} %w_hbm.3), custom_call_target="tpu_custom_call" | custom-call | flops 7784628224 | bytes 4194304 | tf_op jit(solution)/shard_map/solve/pallas_call | solution.py:349
  54.0 7.0 %project.1 = bf16[1,1024,2048]{2,1,0:T(8,128)(2,1)} custom-call(bf16[1024,512]{1,0:T(8,128)(2,1)} %get-tuple-element.7.r_ref, bf16[2048,512]{1,0:T(8,128)(2,1)} %w_hbm.3, bf16[3,512,512]{2,1,0:T(8,128)(2,1)} %get-tuple-element.8.pieces_ref), custom_call_target="tpu_custom_call" | custom-call | flops 2147483648 | bytes 4194304 | tf_op jit(solution)/shard_map/project/pallas_call | solution.py:381

commit v3 on v2

--- a/solution.py
+++ b/solution.py
@@ -37,10 +37,10 @@
 def solve_kernel(
     n_seq, n_head,
     k_hbm, v_hbm, q_hbm, g_ref, ridge_ref, w_hbm, out_ref, pieces_ref,
-    k_ref, v_ref, q_ref, keys_t, keys_w, values_w, scales, gram_local, moment_local,
+    k_ref, v_ref, q_ref, gate_columns, keys_t, keys_w, values_w, scales, gram_local, moment_local,
     gram_high, gram_low, direct, res, sol, norms, images,
     own, mate, chip_sum, slots, give, prior,
-    load_sems, piece_sems, mate_sems, send_sems, recv_sems, back_sems,
+    load_sems, piece_sems, plane_sems, chip_sems, mate_sems, send_sems, recv_sems, back_sems,
 ):
     tokens, head_width = k_ref.shape
     heads = head_width // HD
@@ -75,6 +75,10 @@
         target = {"head": lax.rem(group + shift, n_head)}
         pl.semaphore_signal(barrier, inc=1, device_id=target, device_id_type=MESH)
 
+    for c in range(blocks):
+        rows = pl.ds(c * SPAN, SPAN)
+        gate_columns[rows, :] = g_ref[:, rows].T
+
     def columns_of(h):
         return pl.ds(pl.multiple_of(h * HD, HD), HD)
 
@@ -88,7 +92,7 @@
                 keys = k_ref[rows, columns_of(h)]
                 keys_f = keys.astype(f32)
                 s = lax.rsqrt(row_sum(keys_f * keys_f) + EPS)
-                gates = g_ref[rows, :]
+                gates = gate_columns[rows, :]
                 gate = row_sum(jnp.where(lax.broadcasted_iota(jnp.int32, gates.shape, 1) == h, gates, 0.0))
                 w_value = gate * s
                 high, low = two_terms(keys_f * (w_value * s))
@@ -142,13 +146,32 @@
             device_id=mate_at, device_id_type=MESH,
         )
 
+    part = head_width // n_seq
+
     def to_head(shift):
         target = lax.rem(group + shift, n_head)
-        return pltpu.make_async_remote_copy(
-            src_ref=w_hbm.at[pl.ds(pl.multiple_of(target * head_width, head_width), head_width)],
-            dst_ref=pieces_ref.at[shift - 1],
+        start = pl.multiple_of(target * head_width + me * part, part)
+        return pltpu.make_async_remote_copy(
+            src_ref=w_hbm.at[pl.ds(start, part)], dst_ref=pieces_ref.at[shift - 1, pair, side],
             send_sem=piece_sems.at[0, shift - 1], recv_sem=piece_sems.at[1, shift - 1],
             device_id={"head": target}, device_id_type=MESH,
+        )
+
+    def to_plane(off):
+        mine_part = pieces_ref.at[:, pair, side]
+        target = {"seq": lax.rem(pair + off, pairs) * 2 + side}
+        return pltpu.make_async_remote_copy(
+            src_ref=mine_part, dst_ref=mine_part,
+            send_sem=plane_sems.at[0, off - 1], recv_sem=plane_sems.at[1, off - 1],
+            device_id=target, device_id_type=MESH,
+        )
+
+    def to_chip():
+        mine_parts = pieces_ref.at[:, :, side]
+        return pltpu.make_async_remote_copy(
+            src_ref=mine_parts, dst_ref=mine_parts,
+            send_sem=chip_sems.at[0], recv_sem=chip_sems.at[1],
+            device_id=mate_at, device_id_type=MESH,
         )
 
     def pass_on(kind):
@@ -186,6 +209,10 @@
     pass_on(MOMENT)
     loads[2].wait()
     collect(GRAM)
+    for shift in range(1, n_head):
+        to_head(shift).wait_recv()
+    for off in range(1, pairs):
+        to_plane(off).start()
 
     def apply(n, at, d, high_ref, low_ref, right_ref, fine=True):
         half_right = jnp.concatenate([high_ref[n], keys_t[at]], 1)
@@ -277,6 +304,9 @@
         @pl.when(p == 0)
         def _():
             collect(MOMENT)
+            for off in range(1, pairs):
+                to_plane(off).wait_recv()
+            to_chip().start()
 
         @pl.when(p == 1)
         def _():
@@ -304,7 +334,10 @@
             def _():
                 to_later(kind, off).wait_send()
     for shift in range(1, n_head):
-        to_head(shift).wait()
+        to_head(shift).wait_send()
+    for off in range(1, pairs):
+        to_plane(off).wait_send()
+    to_chip().wait()
 
 
 def project_kernel(r_ref, w_hbm, pieces_ref, out_ref, weight, sems):
@@ -352,10 +385,11 @@
         out_specs=[in_vmem, hbm],
         out_shape=[
             jax.ShapeDtypeStruct((tokens, head_width), bf16),
-            jax.ShapeDtypeStruct((n_head - 1, head_width, width), bf16),
+            jax.ShapeDtypeStruct((n_head - 1, pairs, 2, head_width // n_seq, width), bf16),
         ],
         scratch_shapes=[
             *[pltpu.VMEM((tokens, head_width), bf16)] * 3,
+            pltpu.VMEM((tokens, heads), f32),
             *[square(every, dtype=bf16)] * 3,
             *[square(every)] * 3,
             *[square(some, dtype=bf16)] * 2,
@@ -364,6 +398,8 @@
             square(2, half), square(2, half), square(2, pairs - 1, half), square(2, half), square(2, 2, half),
             pltpu.SemaphoreType.DMA((3,)),
             pltpu.SemaphoreType.DMA((2, n_head - 1)),
+            pltpu.SemaphoreType.DMA((2, pairs - 1)),
+            pltpu.SemaphoreType.DMA((2,)),
             pltpu.SemaphoreType.DMA((2, 2)),
             pltpu.SemaphoreType.DMA((2, pairs - 1)),
             pltpu.SemaphoreType.DMA((2, pairs - 1)),
@@ -376,7 +412,7 @@
             flops=heads * blocks * 58 * tile, bytes_accessed=tokens * head_width * 8, transcendentals=0
         ),
         name="solve",
-    )(keys, values, queries, gates, ridge, out_weight)
+    )(keys, values, queries, gates.T, ridge, out_weight)
     rows = 2 * SPAN
     return pl.pallas_call(
         project_kernel,
@@ -395,7 +431,7 @@
             transcendentals=0,
         ),
         name="project",
-    )(readout, out_weight, pieces)
+    )(readout, out_weight, pieces.reshape(n_head - 1, head_width, width))
 
 
 def solution(mesh):

time: 61.4 us -> 49.6 us (0.81)
  the two profiles are of different devices: /device:TPU:8 before, /device:TPU:2 now
where the time goes in v3:
time: 49.6 us; the launch traced here: 49.3 us
  Pallas kernels  49.3 us (99%)
    pallas_call x1, Pallas kernels, shards(): pl.pallas_call(functools.partial(solve_kernel, n_seq, n_head), in_specs=[...  42.3 us
    pallas_call x1, Pallas kernels, shards(): pl.pallas_call(project_kernel, grid=(tokens // rows,), in_specs=[pl.Block...  7.03 us

profile of v3, /device:TPU:2, one launch (start us, length us, event | category | flops | bytes accessed | tf_op | source)
XLA Modules:
  0.0 49.3 jit_solution(17899165690131968413)
XLA Ops:
  0.0 42.3 %solve.1 = (bf16[1024,512]{1,0:T(8,128)(2,1)}, bf16[3,4,2,64,512]{4,3,2,1,0:T(8,128)(2,1)}) custom-call(bf16[1024,512]{1,0:T(8,128)(2,1)} %k_hbm.1, bf16[1024,512]{1,0:T(8,128)(2,1)} %v_hbm.1, bf16[1024,512]{1,0:T(8,128)(2,1)} %q_hbm.1, f32[4,1024]{1,0:T(4,128)} %bitcast.3, f32[4]{0:T(128)} %ridge_ref.1, bf16[2048,512]{1,0:T(8,128)(2,1)} %w_hbm.3), custom_call_target="tpu_custom_call" | custom-call | flops 7784628224 | bytes 4194304 | tf_op jit(solution)/shard_map/solve/pallas_call | solution.py:382
  42.3 7.0 %project.1 = bf16[1,1024,2048]{2,1,0:T(8,128)(2,1)} custom-call(bf16[1024,512]{1,0:T(8,128)(2,1)} %get-tuple-element.7.r_ref, bf16[2048,512]{1,0:T(8,128)(2,1)} %w_hbm.3, bf16[3,512,512]{2,1,0:T(8,128)(2,1)} %bitcast.2), custom_call_target="tpu_custom_call" | custom-call | flops 2147483648 | bytes 4194304 | tf_op jit(solution)/shard_map/project/pallas_call | solution.py:417

commit v4 on v2

--- a/solution.py
+++ b/solution.py
@@ -37,10 +37,10 @@
 def solve_kernel(
     n_seq, n_head,
     k_hbm, v_hbm, q_hbm, g_ref, ridge_ref, w_hbm, out_ref, pieces_ref,
-    k_ref, v_ref, q_ref, keys_t, keys_w, values_w, scales, gram_local, moment_local,
+    k_ref, v_ref, q_ref, gate_columns, keys_t, keys_w, values_w, scales, gram_local, moment_local,
     gram_high, gram_low, direct, res, sol, norms, images,
     own, mate, chip_sum, slots, give, prior,
-    load_sems, piece_sems, mate_sems, send_sems, recv_sems, back_sems,
+    load_sems, piece_sems, plane_sems, chip_sems, mate_sems, send_sems, recv_sems, back_sems,
 ):
     tokens, head_width = k_ref.shape
     heads = head_width // HD
@@ -75,6 +75,10 @@
         target = {"head": lax.rem(group + shift, n_head)}
         pl.semaphore_signal(barrier, inc=1, device_id=target, device_id_type=MESH)
 
+    for c in range(blocks):
+        rows = pl.ds(c * SPAN, SPAN)
+        gate_columns[rows, :] = g_ref[:, rows].T
+
     def columns_of(h):
         return pl.ds(pl.multiple_of(h * HD, HD), HD)
 
@@ -88,7 +92,7 @@
                 keys = k_ref[rows, columns_of(h)]
                 keys_f = keys.astype(f32)
                 s = lax.rsqrt(row_sum(keys_f * keys_f) + EPS)
-                gates = g_ref[rows, :]
+                gates = gate_columns[rows, :]
                 gate = row_sum(jnp.where(lax.broadcasted_iota(jnp.int32, gates.shape, 1) == h, gates, 0.0))
                 w_value = gate * s
                 high, low = two_terms(keys_f * (w_value * s))
@@ -142,13 +146,34 @@
             device_id=mate_at, device_id_type=MESH,
         )
 
+    part = pieces_ref.shape[3]
+    across = (pair + 1 - 2 * lax.rem(pair, 2), pair + 2 - 4 * lax.rem(pair // 2, 2))
+    quarter = 2 * lax.rem(pair + pair // 2, 2)
+
     def to_head(shift):
         target = lax.rem(group + shift, n_head)
-        return pltpu.make_async_remote_copy(
-            src_ref=w_hbm.at[pl.ds(pl.multiple_of(target * head_width, head_width), head_width)],
-            dst_ref=pieces_ref.at[shift - 1],
+        start = pl.multiple_of(target * head_width + (side * 4 + quarter) * part, part)
+        return pltpu.make_async_remote_copy(
+            src_ref=w_hbm.at[pl.ds(start, 2 * part)].reshape(2, part, w_hbm.shape[1]),
+            dst_ref=pieces_ref.at[shift - 1, side, pl.ds(quarter, 2)],
             send_sem=piece_sems.at[0, shift - 1], recv_sem=piece_sems.at[1, shift - 1],
             device_id={"head": target}, device_id_type=MESH,
+        )
+
+    def to_plane(i):
+        shared = pieces_ref.at[:, side, quarter + i]
+        return pltpu.make_async_remote_copy(
+            src_ref=shared, dst_ref=shared,
+            send_sem=plane_sems.at[0, i], recv_sem=plane_sems.at[1, i],
+            device_id={"seq": across[i] * 2 + side}, device_id_type=MESH,
+        )
+
+    def to_chip(i):
+        shared = pieces_ref.at[:, side, pl.ds(quarter + i * (2 - 2 * quarter), 2)]
+        return pltpu.make_async_remote_copy(
+            src_ref=shared, dst_ref=shared,
+            send_sem=chip_sems.at[0, i], recv_sem=chip_sems.at[1, i],
+            device_id=mate_at, device_id_type=MESH,
         )
 
     def pass_on(kind):
@@ -265,9 +290,24 @@
         for n in range(behind):
             multiply(behind + n)
 
-        def sweep(_, carry):
+        def sweep(i, carry):
             iteration()
             iteration()
+
+            @pl.when((p == 0) & (i == 1))
+            def _():
+                for shift in range(1, n_head):
+                    to_head(shift).wait_recv()
+                for which in range(2):
+                    to_plane(which).start()
+                to_chip(0).start()
+
+            @pl.when((p == 1) & (i == 0))
+            def _():
+                for which in range(2):
+                    to_plane(which).wait_recv()
+                to_chip(1).start()
+
             return carry
 
         lax.fori_loop(0, (ITERS - 2) // 2, sweep, 0)
@@ -304,7 +344,10 @@
             def _():
                 to_later(kind, off).wait_send()
     for shift in range(1, n_head):
-        to_head(shift).wait()
+        to_head(shift).wait_send()
+    for i in range(2):
+        to_plane(i).wait_send()
+        to_chip(i).wait()
 
 
 def project_kernel(r_ref, w_hbm, pieces_ref, out_ref, weight, sems):
@@ -352,10 +395,11 @@
         out_specs=[in_vmem, hbm],
         out_shape=[
             jax.ShapeDtypeStruct((tokens, head_width), bf16),
-            jax.ShapeDtypeStruct((n_head - 1, head_width, width), bf16),
+            jax.ShapeDtypeStruct((n_head - 1, 2, 4, head_width // 8, width), bf16),
         ],
         scratch_shapes=[
             *[pltpu.VMEM((tokens, head_width), bf16)] * 3,
+            pltpu.VMEM((tokens, heads), f32),
             *[square(every, dtype=bf16)] * 3,
             *[square(every)] * 3,
             *[square(some, dtype=bf16)] * 2,
@@ -364,6 +408,8 @@
             square(2, half), square(2, half), square(2, pairs - 1, half), square(2, half), square(2, 2, half),
             pltpu.SemaphoreType.DMA((3,)),
             pltpu.SemaphoreType.DMA((2, n_head - 1)),
+            pltpu.SemaphoreType.DMA((2, 2)),
+            pltpu.SemaphoreType.DMA((2, 2)),
             pltpu.SemaphoreType.DMA((2, 2)),
             pltpu.SemaphoreType.DMA((2, pairs - 1)),
             pltpu.SemaphoreType.DMA((2, pairs - 1)),
@@ -376,7 +422,7 @@
             flops=heads * blocks * 58 * tile, bytes_accessed=tokens * head_width * 8, transcendentals=0
         ),
         name="solve",
-    )(keys, values, queries, gates, ridge, out_weight)
+    )(keys, values, queries, gates.T, ridge, out_weight)
     rows = 2 * SPAN
     return pl.pallas_call(
         project_kernel,
@@ -395,7 +441,7 @@
             transcendentals=0,
         ),
         name="project",
-    )(readout, out_weight, pieces)
+    )(readout, out_weight, pieces.reshape(n_head - 1, head_width, width))
 
 
 def solution(mesh):

time: 61.4 us -> 43.8 us (0.71)
  the two profiles are of different devices: /device:TPU:8 before, /device:TPU:4 now
where the time goes in v4:
time: 43.8 us; the launch traced here: 43.6 us
  Pallas kernels  43.5 us (99%)
    pallas_call x1, Pallas kernels, shards(): pl.pallas_call(functools.partial(solve_kernel, n_seq, n_head), in_specs=[...  36.5 us
    pallas_call x1, Pallas kernels, shards(): pl.pallas_call(project_kernel, grid=(tokens // rows,), in_specs=[pl.Block...  7.04 us

profile of v4, /device:TPU:4, one launch (start us, length us, event | category | flops | bytes accessed | tf_op | source)
XLA Modules:
  0.0 43.6 jit_solution(14095313555459705874)
XLA Ops:
  0.0 36.5 %solve.1 = (bf16[1024,512]{1,0:T(8,128)(2,1)}, bf16[3,2,4,64,512]{4,3,2,1,0:T(8,128)(2,1)}) custom-call(bf16[1024,512]{1,0:T(8,128)(2,1)} %k_hbm.1, bf16[1024,512]{1,0:T(8,128)(2,1)} %v_hbm.1, bf16[1024,512]{1,0:T(8,128)(2,1)} %q_hbm.1, f32[4,1024]{1,0:T(4,128)} %bitcast.3, f32[4]{0:T(128)} %ridge_ref.1, bf16[2048,512]{1,0:T(8,128)(2,1)} %w_hbm.3), custom_call_target="tpu_custom_call" | custom-call | flops 7784628224 | bytes 4194304 | tf_op jit(solution)/shard_map/solve/pallas_call | solution.py:392
  36.5 7.0 %project.1 = bf16[1,1024,2048]{2,1,0:T(8,128)(2,1)} custom-call(bf16[1024,512]{1,0:T(8,128)(2,1)} %get-tuple-element.7.r_ref, bf16[2048,512]{1,0:T(8,128)(2,1)} %w_hbm.3, bf16[3,512,512]{2,1,0:T(8,128)(2,1)} %bitcast.2), custom_call_target="tpu_custom_call" | custom-call | flops 2147483648 | bytes 4194304 | tf_op jit(solution)/shard_map/project/pallas_call | solution.py:427

commit v5 on v4

--- a/solution.py
+++ b/solution.py
@@ -39,7 +39,7 @@
     k_hbm, v_hbm, q_hbm, g_ref, ridge_ref, w_hbm, out_ref, pieces_ref,
     k_ref, v_ref, q_ref, gate_columns, keys_t, keys_w, values_w, scales, gram_local, moment_local,
     gram_high, gram_low, direct, res, sol, norms, images,
-    own, mate, chip_sum, slots, give, prior,
+    own, mate, chip_gram, chip_moment, gram_slots, moment_slots, give, prior,
     load_sems, piece_sems, plane_sems, chip_sems, mate_sems, send_sems, recv_sems, back_sems,
 ):
     tokens, head_width = k_ref.shape
@@ -58,6 +58,7 @@
     col = lax.broadcasted_iota(jnp.int32, (HD, HD), 1)
     causal = (col <= row).astype(f32).astype(bf16)
     GRAM, MOMENT = 0, 1
+    chip_sums, slots = (chip_gram, chip_moment), (gram_slots, moment_slots)
 
     loads = [
         pltpu.make_async_copy(src, dst, load_sems.at[i])
@@ -134,7 +135,7 @@
     def to_later(kind, off):
         target = {"seq": lax.rem(pair + off, pairs) * 2 + side}
         return pltpu.make_async_remote_copy(
-            src_ref=chip_sum.at[kind], dst_ref=slots.at[kind, off - 1],
+            src_ref=chip_sums[kind], dst_ref=slots[kind].at[off - 1],
             send_sem=send_sems.at[kind, off - 1], recv_sem=recv_sems.at[kind, off - 1],
             device_id=target, device_id_type=MESH,
         )
@@ -178,7 +179,8 @@
 
     def pass_on(kind):
         to_mate(kind).wait_recv()
-        chip_sum[kind] = own[kind, pl.ds(mine, half)] + mate[kind]
+        chip = own[kind, pl.ds(mine, half)] + mate[kind]
+        chip_sums[kind][...] = chip.astype(chip_sums[kind].dtype)
         for off in range(1, pairs):
             @pl.when(pair + off < pairs)
             def _():
@@ -191,7 +193,7 @@
             @pl.when(pair >= off)
             def _():
                 to_later(kind, off).wait_recv()
-                give[kind] = give[kind] + slots[kind, off - 1]
+                give[kind] = give[kind] + slots[kind][off - 1].astype(f32)
         prior[kind, 0] = give[kind] + side.astype(f32) * mate[kind]
         give[kind] = give[kind] + (1 - side).astype(f32) * own[kind, pl.ds(mine, half)]
         to_back(kind).start()
@@ -200,15 +202,14 @@
     sum_grams(others)
     pl.semaphore_wait(barrier, pairs + n_head - 1)
     to_mate(GRAM).start()
+    sum_grams(mine)
+    pass_on(GRAM)
     for shift in range(1, n_head):
         to_head(shift).start()
-    sum_grams(mine)
-    pass_on(GRAM)
     loads[1].wait()
     sum_moments(others)
     to_mate(MOMENT).start()
     sum_moments(mine)
-    pass_on(MOMENT)
     loads[2].wait()
     collect(GRAM)
 
@@ -294,15 +295,11 @@
             iteration()
             iteration()
 
-            @pl.when((p == 0) & (i == 1))
+            @pl.when((p == 0) & (i == 0))
             def _():
-                for shift in range(1, n_head):
-                    to_head(shift).wait_recv()
-                for which in range(2):
-                    to_plane(which).start()
-                to_chip(0).start()
-
-            @pl.when((p == 1) & (i == 0))
+                pass_on(MOMENT)
+
+            @pl.when((p == 1) & (i == 2))
             def _():
                 for which in range(2):
                     to_plane(which).wait_recv()
@@ -317,6 +314,11 @@
         @pl.when(p == 0)
         def _():
             collect(MOMENT)
+            for shift in range(1, n_head):
+                to_head(shift).wait_recv()
+            for which in range(2):
+                to_plane(which).start()
+            to_chip(0).start()
 
         @pl.when(p == 1)
         def _():
@@ -405,7 +407,9 @@
             *[square(some, dtype=bf16)] * 2,
             *[square(some)] * 5,
             square(2, heads),
-            square(2, half), square(2, half), square(2, pairs - 1, half), square(2, half), square(2, 2, half),
+            square(2, half), square(half), square(half, dtype=bf16),
+            square(pairs - 1, half), square(pairs - 1, half, dtype=bf16),
+            square(2, half), square(2, 2, half),
             pltpu.SemaphoreType.DMA((3,)),
             pltpu.SemaphoreType.DMA((2, n_head - 1)),
             pltpu.SemaphoreType.DMA((2, 2)),

time: 43.8 us -> 40.9 us (0.934)
  the two profiles are of different devices: /device:TPU:4 before, /device:TPU:7 now
where the time goes in v5:
time: 40.9 us; the launch traced here: 40.2 us
  Pallas kernels  40.2 us (98%)
    pallas_call x1, Pallas kernels, shards(): pl.pallas_call(functools.partial(solve_kernel, n_seq, n_head), in_specs=[...  33.1 us
    pallas_call x1, Pallas kernels, shards(): pl.pallas_call(project_kernel, grid=(tokens // rows,), in_specs=[pl.Block...  7.03 us

profile of v5, /device:TPU:7, one launch (start us, length us, event | category | flops | bytes accessed | tf_op | source)
XLA Modules:
  0.0 40.2 jit_solution(17738186938867173173)
XLA Ops:
  0.0 33.1 %solve.1 = (bf16[1024,512]{1,0:T(8,128)(2,1)}, bf16[3,2,4,64,512]{4,3,2,1,0:T(8,128)(2,1)}) custom-call(bf16[1024,512]{1,0:T(8,128)(2,1)} %k_hbm.1, bf16[1024,512]{1,0:T(8,128)(2,1)} %v_hbm.1, bf16[1024,512]{1,0:T(8,128)(2,1)} %q_hbm.1, f32[4,1024]{1,0:T(4,128)} %bitcast.3, f32[4]{0:T(128)} %ridge_ref.1, bf16[2048,512]{1,0:T(8,128)(2,1)} %w_hbm.3), custom_call_target="tpu_custom_call" | custom-call | flops 7784628224 | bytes 4194304 | tf_op jit(solution)/shard_map/solve/pallas_call | solution.py:394
  33.1 7.0 %project.1 = bf16[1,1024,2048]{2,1,0:T(8,128)(2,1)} custom-call(bf16[1024,512]{1,0:T(8,128)(2,1)} %get-tuple-element.7.r_ref, bf16[2048,512]{1,0:T(8,128)(2,1)} %w_hbm.3, bf16[3,512,512]{2,1,0:T(8,128)(2,1)} %bitcast.2), custom_call_target="tpu_custom_call" | custom-call | flops 2147483648 | bytes 4194304 | tf_op jit(solution)/shard_map/project/pallas_call | solution.py:431

commit v6 on v5

--- a/solution.py
+++ b/solution.py
@@ -15,6 +15,7 @@
 bf16 = jnp.bfloat16
 VMEM_BYTES = 56 * 1024 * 1024
 MESH = pl.DeviceIdType.MESH
+PROJECT_ROWS = 256
 
 
 def dot(a, b):
@@ -352,28 +353,40 @@
         to_chip(i).wait()
 
 
-def project_kernel(r_ref, w_hbm, pieces_ref, out_ref, weight, sems):
-    count = pieces_ref.shape[0] + 1
-    depth, width = pieces_ref.shape[1:]
+def project_kernel(r_hbm, w_hbm, pieces_ref, out_ref, readout, weight, result, in_sems, out_sems):
+    count, depth, width = weight.shape
+    tokens = readout.shape[0]
+    rows = tokens // out_sems.shape[1]
     me = lax.axis_index("head")
 
-    @pl.when(pl.program_id(0) == 0)
-    def _():
-        copies = []
-        for shift in range(count):
-            owner = lax.rem(me + count - shift, count)
-            if shift:
-                source = pieces_ref.at[shift - 1]
-            else:
-                source = w_hbm.at[pl.ds(pl.multiple_of(me * depth, depth), depth)]
-            columns = pl.ds(pl.multiple_of(owner * width, width), width)
-            copies.append(pltpu.make_async_copy(source, weight.at[:, columns], sems.at[shift]))
-        for copy in copies:
-            copy.start()
-        for copy in copies:
-            copy.wait()
-
-    out_ref[0] = dot(r_ref[...], weight[...]).astype(out_ref.dtype)
+    def fetch(shift):
+        if shift:
+            source = pieces_ref.at[shift - 1]
+        else:
+            source = w_hbm.at[pl.ds(pl.multiple_of(me * depth, depth), depth)]
+        return pltpu.make_async_copy(source, weight.at[shift], in_sems.at[shift])
+
+    load = pltpu.make_async_copy(r_hbm, readout, in_sems.at[count])
+    load.start()
+    for shift in range(count):
+        fetch(shift).start()
+    load.wait()
+    stores = []
+    for shift in range(count):
+        fetch(shift).wait()
+        owner = lax.rem(me + count - shift, count)
+        columns = pl.ds(pl.multiple_of(owner * width, width), width)
+        for block in range(tokens // rows):
+            part = pl.ds(block * rows, rows)
+            result[shift, part] = dot(readout[part], weight[shift]).astype(result.dtype)
+            stores.append(
+                pltpu.make_async_copy(
+                    result.at[shift, part], out_ref.at[0, part, columns], out_sems.at[shift, block]
+                )
+            )
+            stores[-1].start()
+    for store in stores:
+        store.wait()
 
 
 def shards(n_seq, n_head, queries, keys, values, gates, ridge, out_weight):
@@ -427,16 +440,17 @@
         ),
         name="solve",
     )(keys, values, queries, gates.T, ridge, out_weight)
-    rows = 2 * SPAN
     return pl.pallas_call(
         project_kernel,
-        grid=(tokens // rows,),
-        in_specs=[pl.BlockSpec((rows, head_width), lambda i: (i, 0)), hbm, hbm],
-        out_specs=pl.BlockSpec((1, rows, width * n_head), lambda i: (0, i, 0)),
+        in_specs=[hbm] * 3,
+        out_specs=hbm,
         out_shape=jax.ShapeDtypeStruct((1, tokens, width * n_head), bf16),
         scratch_shapes=[
-            pltpu.VMEM((head_width, width * n_head), bf16),
-            pltpu.SemaphoreType.DMA((n_head,)),
+            pltpu.VMEM((tokens, head_width), bf16),
+            pltpu.VMEM((n_head, head_width, width), bf16),
+            pltpu.VMEM((n_head, tokens, width), bf16),
+            pltpu.SemaphoreType.DMA((n_head + 1,)),
+            pltpu.SemaphoreType.DMA((n_head, tokens // PROJECT_ROWS)),
         ],
         compiler_params=pltpu.CompilerParams(vmem_limit_bytes=VMEM_BYTES),
         cost_estimate=pl.CostEstimate(

time: 40.9 us -> 38.9 us (0.951)
  Pallas kernels: 40.2 us -> 38.2 us
    pallas_call x1, Pallas kernels: 7.03 us -> 5.1 us  [shards(): pl.pallas_call(project_kernel, in_specs=[hbm] * 3, out_specs=hbm, out_sha...]
where the time goes in v6:
time: 38.9 us; the launch traced here: 38.2 us
  Pallas kernels  38.2 us (98%)
    pallas_call x1, Pallas kernels, shards(): pl.pallas_call(functools.partial(solve_kernel, n_seq, n_head), in_specs=[...  33.1 us
    pallas_call x1, Pallas kernels, shards(): pl.pallas_call(project_kernel, in_specs=[hbm] * 3, out_specs=hbm, out_sha...  5.1 us

profile of v6, /device:TPU:7, one launch (start us, length us, event | category | flops | bytes accessed | tf_op | source)
XLA Modules:
  0.0 38.2 jit_solution(12866511770848013579)
XLA Ops:
  0.0 33.1 %solve.1 = (bf16[1024,512]{1,0:T(8,128)(2,1)}, bf16[3,2,4,64,512]{4,3,2,1,0:T(8,128)(2,1)}) custom-call(bf16[1024,512]{1,0:T(8,128)(2,1)} %k_hbm.1, bf16[1024,512]{1,0:T(8,128)(2,1)} %v_hbm.1, bf16[1024,512]{1,0:T(8,128)(2,1)} %q_hbm.1, f32[4,1024]{1,0:T(4,128)} %bitcast.3, f32[4]{0:T(128)} %ridge_ref.1, bf16[2048,512]{1,0:T(8,128)(2,1)} %w_hbm.3), custom_call_target="tpu_custom_call" | custom-call | flops 7784628224 | bytes 4194304 | tf_op jit(solution)/shard_map/solve/pallas_call | solution.py:407
  33.1 5.1 %project.1 = bf16[1,1024,2048]{2,1,0:T(8,128)(2,1)} custom-call(bf16[1024,512]{1,0:T(8,128)(2,1)} %get-tuple-element.7.r_hbm, bf16[2048,512]{1,0:T(8,128)(2,1)} %w_hbm.3, bf16[3,512,512]{2,1,0:T(8,128)(2,1)} %bitcast.2), custom_call_target="tpu_custom_call" | custom-call | flops 2147483648 | bytes 4194304 | tf_op jit(solution)/shard_map/project/pallas_call | solution.py:443

commit v7 on v6

--- a/solution.py
+++ b/solution.py
@@ -53,8 +53,8 @@
     side = lax.rem(me, 2)
     pair = me // 2
     mate_at = {"seq": me + 1 - 2 * side}
-    mine = side * half
-    others = (1 - side) * half
+    mine = pl.ds(pl.multiple_of(side * (HD // 2), HD // 2), HD // 2)
+    others = pl.ds(pl.multiple_of((1 - side) * (HD // 2), HD // 2), HD // 2)
     row = lax.broadcasted_iota(jnp.int32, (HD, HD), 0)
     col = lax.broadcasted_iota(jnp.int32, (HD, HD), 1)
     causal = (col <= row).astype(f32).astype(bf16)
@@ -126,25 +126,28 @@
 
         lax.fori_loop(0, half, one, 0)
 
-    def to_mate(kind):
+    def heads_of(p):
+        return pl.ds(p * half, half)
+
+    def to_mate(kind, p):
         return pltpu.make_async_remote_copy(
-            src_ref=own.at[kind, pl.ds(others, half)], dst_ref=mate.at[kind],
-            send_sem=mate_sems.at[kind, 0], recv_sem=mate_sems.at[kind, 1],
+            src_ref=own.at[kind, heads_of(p), others], dst_ref=mate.at[kind, p],
+            send_sem=mate_sems.at[kind, p, 0], recv_sem=mate_sems.at[kind, p, 1],
             device_id=mate_at, device_id_type=MESH,
         )
 
-    def to_later(kind, off):
+    def to_later(kind, p, off):
         target = {"seq": lax.rem(pair + off, pairs) * 2 + side}
         return pltpu.make_async_remote_copy(
-            src_ref=chip_sums[kind], dst_ref=slots[kind].at[off - 1],
-            send_sem=send_sems.at[kind, off - 1], recv_sem=recv_sems.at[kind, off - 1],
+            src_ref=chip_sums[kind].at[p], dst_ref=slots[kind].at[p, off - 1],
+            send_sem=send_sems.at[kind, p, off - 1], recv_sem=recv_sems.at[kind, p, off - 1],
             device_id=target, device_id_type=MESH,
         )
 
-    def to_back(kind):
+    def to_back(kind, p):
         return pltpu.make_async_remote_copy(
-            src_ref=give.at[kind], dst_ref=prior.at[kind, 1],
-            send_sem=back_sems.at[kind, 0], recv_sem=back_sems.at[kind, 1],
+            src_ref=give.at[kind, p], dst_ref=prior.at[kind, heads_of(p), mine],
+            send_sem=back_sems.at[kind, p, 0], recv_sem=back_sems.at[kind, p, 1],
             device_id=mate_at, device_id_type=MESH,
         )
 
@@ -178,41 +181,59 @@
             device_id=mate_at, device_id_type=MESH,
         )
 
-    def pass_on(kind):
-        to_mate(kind).wait_recv()
-        chip = own[kind, pl.ds(mine, half)] + mate[kind]
-        chip_sums[kind][...] = chip.astype(chip_sums[kind].dtype)
+    def pass_on(kind, p):
+        to_mate(kind, p).wait_recv()
+        chip = own[kind, heads_of(p), mine] + mate[kind, p]
+        chip_sums[kind][p] = chip.astype(chip_sums[kind].dtype)
         for off in range(1, pairs):
             @pl.when(pair + off < pairs)
             def _():
-                to_later(kind, off).start()
-
-    def collect(kind):
-        total = jnp.zeros((half, HD, HD), f32)
-        give[kind] = total
+                to_later(kind, p, off).start()
+
+    def collect(kind, p):
+        give[kind, p] = jnp.zeros((half, HD // 2, HD), f32)
         for off in range(1, pairs):
             @pl.when(pair >= off)
             def _():
-                to_later(kind, off).wait_recv()
-                give[kind] = give[kind] + slots[kind][off - 1].astype(f32)
-        prior[kind, 0] = give[kind] + side.astype(f32) * mate[kind]
-        give[kind] = give[kind] + (1 - side).astype(f32) * own[kind, pl.ds(mine, half)]
-        to_back(kind).start()
+                to_later(kind, p, off).wait_recv()
+                give[kind, p] = give[kind, p] + slots[kind][p, off - 1].astype(f32)
+        prior[kind, heads_of(p), mine] = give[kind, p] + side.astype(f32) * mate[kind, p]
+        give[kind, p] = give[kind, p] + (1 - side).astype(f32) * own[kind, heads_of(p), mine]
+        to_back(kind, p).start()
+
+    def start_queries(p):
+        def one(j, carry):
+            for c in range(blocks):
+                n = j * blocks + c
+                queries = q_ref[pl.ds(c * SPAN, SPAN), columns_of(p * half + j)].astype(f32)
+                square = row_sum(queries * queries)
+                scale = lax.rsqrt(square + EPS)
+                queries = queries * scale
+                res[n] = queries
+                direct[n] = queries
+                norms[n] = wide(square * scale * scale)
+            return carry
+
+        lax.fori_loop(0, half, one, 0)
 
     loads[0].wait()
-    sum_grams(others)
+    sum_grams(0)
     pl.semaphore_wait(barrier, pairs + n_head - 1)
-    to_mate(GRAM).start()
-    sum_grams(mine)
-    pass_on(GRAM)
+    to_mate(GRAM, 0).start()
+    sum_grams(half)
+    pass_on(GRAM, 0)
+    to_mate(GRAM, 1).start()
     for shift in range(1, n_head):
         to_head(shift).start()
     loads[1].wait()
-    sum_moments(others)
-    to_mate(MOMENT).start()
-    sum_moments(mine)
+    sum_moments(0)
+    to_mate(MOMENT, 0).start()
     loads[2].wait()
-    collect(GRAM)
+    start_queries(0)
+    collect(GRAM, 0)
+    sum_moments(half)
+    to_mate(MOMENT, 1).start()
+    to_back(GRAM, 0).wait_recv()
 
     def apply(n, at, d, high_ref, low_ref, right_ref, fine=True):
         half_right = jnp.concatenate([high_ref[n], keys_t[at]], 1)
@@ -235,30 +256,23 @@
     behind = units // 2
 
     def run(p, carry):
-        first = mine + p * (others - mine)
+        first = p * half
 
         @pl.when(p == 1)
         def _():
-            to_back(GRAM).wait_recv()
-
-        def split(kind, j, c, local, low_too=None):
-            total = local[(first + j) * blocks + c] + prior[kind, p, j]
+            start_queries(1)
+            to_back(GRAM, 1).wait_recv()
+
+        def split(kind, j, c, local):
+            total = local[(first + j) * blocks + c] + prior[kind, first + j]
             if kind == GRAM:
                 total += jnp.where(row == col, ridge_ref[first + j], 0.0)
             gram_high[j * blocks + c], gram_low[j * blocks + c] = two_terms(total)
 
         def prepare(j, carry):
             for c in range(blocks):
-                n = j * blocks + c
                 split(GRAM, j, c, gram_local)
-                queries = q_ref[pl.ds(c * SPAN, SPAN), columns_of(first + j)].astype(f32)
-                square = row_sum(queries * queries)
-                scale = lax.rsqrt(square + EPS)
-                queries = queries * scale
-                res[n] = queries
-                direct[n] = queries
-                sol[n] = jnp.zeros((SPAN, HD), f32)
-                norms[n] = wide(square * scale * scale)
+                sol[j * blocks + c] = jnp.zeros((SPAN, HD), f32)
             return carry
 
         lax.fori_loop(0, half, prepare, 0)
@@ -298,7 +312,12 @@
 
             @pl.when((p == 0) & (i == 0))
             def _():
-                pass_on(MOMENT)
+                pass_on(GRAM, 1)
+                pass_on(MOMENT, 0)
+
+            @pl.when((p == 0) & (i == 2))
+            def _():
+                pass_on(MOMENT, 1)
 
             @pl.when((p == 1) & (i == 2))
             def _():
@@ -310,20 +329,27 @@
 
         lax.fori_loop(0, (ITERS - 2) // 2, sweep, 0)
         iteration(before_last=True)
-        iteration(last=True)
 
         @pl.when(p == 0)
         def _():
-            collect(MOMENT)
+            collect(MOMENT, 0)
+            collect(GRAM, 1)
+
+        @pl.when(p == 1)
+        def _():
+            collect(MOMENT, 1)
+
+        iteration(last=True)
+
+        @pl.when(p == 0)
+        def _():
             for shift in range(1, n_head):
                 to_head(shift).wait_recv()
             for which in range(2):
                 to_plane(which).start()
             to_chip(0).start()
 
-        @pl.when(p == 1)
-        def _():
-            to_back(MOMENT).wait_recv()
+        to_back(MOMENT, p).wait_recv()
 
         def finish(j, carry):
             for c in range(blocks):
@@ -340,12 +366,13 @@
 
     lax.fori_loop(0, 2, run, 0)
     for kind in (GRAM, MOMENT):
-        to_mate(kind).wait_send()
-        to_back(kind).wait_send()
-        for off in range(1, pairs):
-            @pl.when(pair + off < pairs)
-            def _():
-                to_later(kind, off).wait_send()
+        for p in range(2):
+            to_mate(kind, p).wait_send()
+            to_back(kind, p).wait_send()
+            for off in range(1, pairs):
+                @pl.when(pair + off < pairs)
+                def _():
+                    to_later(kind, p, off).wait_send()
     for shift in range(1, n_head):
         to_head(shift).wait_send()
     for i in range(2):
@@ -403,6 +430,9 @@
     def square(*lead, dtype=f32):
         return pltpu.VMEM((*lead, HD, HD), dtype)
 
+    def strip(*lead, dtype=f32):
+        return pltpu.VMEM((*lead, HD // 2, HD), dtype)
+
     every, some = heads * blocks, half * blocks
     readout, pieces = pl.pallas_call(
         functools.partial(solve_kernel, n_seq, n_head),
@@ -420,17 +450,17 @@
             *[square(some, dtype=bf16)] * 2,
             *[square(some)] * 5,
             square(2, heads),
-            square(2, half), square(half), square(half, dtype=bf16),
-            square(pairs - 1, half), square(pairs - 1, half, dtype=bf16),
-            square(2, half), square(2, 2, half),
+            strip(2, 2, half), strip(2, half), strip(2, half, dtype=bf16),
+            strip(2, pairs - 1, half), strip(2, pairs - 1, half, dtype=bf16),
+            strip(2, 2, half), square(2, heads),
             pltpu.SemaphoreType.DMA((3,)),
             pltpu.SemaphoreType.DMA((2, n_head - 1)),
             pltpu.SemaphoreType.DMA((2, 2)),
             pltpu.SemaphoreType.DMA((2, 2)),
-            pltpu.SemaphoreType.DMA((2, 2)),
-            pltpu.SemaphoreType.DMA((2, pairs - 1)),
-            pltpu.SemaphoreType.DMA((2, pairs - 1)),
-            pltpu.SemaphoreType.DMA((2, 2)),
+            pltpu.SemaphoreType.DMA((2, 2, 2)),
+            pltpu.SemaphoreType.DMA((2, 2, pairs - 1)),
+            pltpu.SemaphoreType.DMA((2, 2, pairs - 1)),
+            pltpu.SemaphoreType.DMA((2, 2, 2)),
         ],
         compiler_params=pltpu.CompilerParams(
             vmem_limit_bytes=VMEM_BYTES, collective_id=0, has_side_effects=True

time: 38.9 us -> 37.6 us (0.967); the launches traced: 38.2 us -> 37.4 us
  Pallas kernels: 38.2 us -> 37.3 us
    pallas_call x1, Pallas kernels: 33.1 us -> 32.2 us  [shards(): pl.pallas_call(functools.partial(solve_kernel, n_seq, n_head), in_specs=[...]
where the time goes in v7:
time: 37.6 us; the launch traced here: 37.4 us
  Pallas kernels  37.3 us (99%)
    pallas_call x1, Pallas kernels, shards(): pl.pallas_call(functools.partial(solve_kernel, n_seq, n_head), in_specs=[...  32.2 us
    pallas_call x1, Pallas kernels, shards(): pl.pallas_call(project_kernel, in_specs=[hbm] * 3, out_specs=hbm, out_sha...  5.1 us

profile of v7, /device:TPU:7, one launch (start us, length us, event | category | flops | bytes accessed | tf_op | source)
XLA Modules:
  0.0 37.4 jit_solution(7061467499686432967)
XLA Ops:
  0.0 32.2 %solve.1 = (bf16[1024,512]{1,0:T(8,128)(2,1)}, bf16[3,2,4,64,512]{4,3,2,1,0:T(8,128)(2,1)}) custom-call(bf16[1024,512]{1,0:T(8,128)(2,1)} %k_hbm.1, bf16[1024,512]{1,0:T(8,128)(2,1)} %v_hbm.1, bf16[1024,512]{1,0:T(8,128)(2,1)} %q_hbm.1, f32[4,1024]{1,0:T(4,128)} %bitcast.3, f32[4]{0:T(128)} %ridge_ref.1, bf16[2048,512]{1,0:T(8,128)(2,1)} %w_hbm.3), custom_call_target="tpu_custom_call" | custom-call | flops 7784628224 | bytes 4194304 | tf_op jit(solution)/shard_map/solve/pallas_call | solution.py:437
  32.3 5.1 %project.1 = bf16[1,1024,2048]{2,1,0:T(8,128)(2,1)} custom-call(bf16[1024,512]{1,0:T(8,128)(2,1)} %get-tuple-element.7.r_hbm, bf16[2048,512]{1,0:T(8,128)(2,1)} %w_hbm.3, bf16[3,512,512]{2,1,0:T(8,128)(2,1)} %bitcast.2), custom_call_target="tpu_custom_call" | custom-call | flops 2147483648 | bytes 4194304 | tf_op jit(solution)/shard_map/project/pallas_call | solution.py:473

commit v8 on v7

--- a/solution.py
+++ b/solution.py
@@ -14,6 +14,7 @@
 f32 = jnp.float32
 bf16 = jnp.bfloat16
 VMEM_BYTES = 56 * 1024 * 1024
+PROJECT_BYTES = 16 * 1024 * 1024
 MESH = pl.DeviceIdType.MESH
 PROJECT_ROWS = 256
 
@@ -380,32 +381,26 @@
         to_chip(i).wait()
 
 
-def project_kernel(r_hbm, w_hbm, pieces_ref, out_ref, readout, weight, result, in_sems, out_sems):
-    count, depth, width = weight.shape
-    tokens = readout.shape[0]
+def project_kernel(readout, w_hbm, pieces_ref, out_ref, weight, result, in_sem, out_sems):
+    count, tokens, width = result.shape
+    depth = readout.shape[1]
     rows = tokens // out_sems.shape[1]
     me = lax.axis_index("head")
-
-    def fetch(shift):
+    own = w_hbm.at[pl.ds(pl.multiple_of(me * depth, depth), depth)]
+    fetch = pltpu.make_async_copy(own, weight, in_sem)
+    fetch.start()
+    stores = []
+    for shift in (*range(1, count), 0):
         if shift:
-            source = pieces_ref.at[shift - 1]
+            piece = pieces_ref[shift - 1].reshape(depth, width)
         else:
-            source = w_hbm.at[pl.ds(pl.multiple_of(me * depth, depth), depth)]
-        return pltpu.make_async_copy(source, weight.at[shift], in_sems.at[shift])
-
-    load = pltpu.make_async_copy(r_hbm, readout, in_sems.at[count])
-    load.start()
-    for shift in range(count):
-        fetch(shift).start()
-    load.wait()
-    stores = []
-    for shift in range(count):
-        fetch(shift).wait()
+            fetch.wait()
+            piece = weight[...]
         owner = lax.rem(me + count - shift, count)
         columns = pl.ds(pl.multiple_of(owner * width, width), width)
         for block in range(tokens // rows):
             part = pl.ds(block * rows, rows)
-            result[shift, part] = dot(readout[part], weight[shift]).astype(result.dtype)
+            result[shift, part] = dot(readout[part], piece).astype(result.dtype)
             stores.append(
                 pltpu.make_async_copy(
                     result.at[shift, part], out_ref.at[0, part, columns], out_sems.at[shift, block]
@@ -437,10 +432,10 @@
     readout, pieces = pl.pallas_call(
         functools.partial(solve_kernel, n_seq, n_head),
         in_specs=[hbm, hbm, hbm, in_vmem, pl.BlockSpec(memory_space=pltpu.SMEM), hbm],
-        out_specs=[in_vmem, hbm],
+        out_specs=[in_vmem, in_vmem],
         out_shape=[
-            jax.ShapeDtypeStruct((tokens, head_width), bf16),
-            jax.ShapeDtypeStruct((n_head - 1, 2, 4, head_width // 8, width), bf16),
+            pltpu.VMEM((tokens, head_width), bf16),
+            pltpu.VMEM((n_head - 1, 2, 4, head_width // 8, width), bf16),
         ],
         scratch_shapes=[
             *[pltpu.VMEM((tokens, head_width), bf16)] * 3,
@@ -472,24 +467,23 @@
     )(keys, values, queries, gates.T, ridge, out_weight)
     return pl.pallas_call(
         project_kernel,
-        in_specs=[hbm] * 3,
+        in_specs=[in_vmem, hbm, in_vmem],
         out_specs=hbm,
         out_shape=jax.ShapeDtypeStruct((1, tokens, width * n_head), bf16),
         scratch_shapes=[
-            pltpu.VMEM((tokens, head_width), bf16),
-            pltpu.VMEM((n_head, head_width, width), bf16),
+            pltpu.VMEM((head_width, width), bf16),
             pltpu.VMEM((n_head, tokens, width), bf16),
-            pltpu.SemaphoreType.DMA((n_head + 1,)),
+            pltpu.SemaphoreType.DMA(()),
             pltpu.SemaphoreType.DMA((n_head, tokens // PROJECT_ROWS)),
         ],
-        compiler_params=pltpu.CompilerParams(vmem_limit_bytes=VMEM_BYTES),
+        compiler_params=pltpu.CompilerParams(vmem_limit_bytes=PROJECT_BYTES),
         cost_estimate=pl.CostEstimate(
             flops=2 * tokens * head_width * width * n_head,
             bytes_accessed=tokens * width * n_head * 2,
             transcendentals=0,
         ),
         name="project",
-    )(readout, out_weight, pieces.reshape(n_head - 1, head_width, width))
+    )(readout, out_weight, pieces)
 
 
 def solution(mesh):

time: 37.6 us -> 34.9 us (0.928)
  Pallas kernels: 37.3 us -> 34.8 us
    pallas_call x1, Pallas kernels: 5.1 us -> 3.41 us  [shards(): pl.pallas_call(project_kernel, in_specs=[in_vmem, hbm, in_vmem], out_spec...]
    pallas_call x1, Pallas kernels: 32.2 us -> 31.3 us  [shards(): pl.pallas_call(functools.partial(solve_kernel, n_seq, n_head), in_specs=[...]
where the time goes in v8:
time: 34.9 us; the launch traced here: 34.8 us
  Pallas kernels  34.8 us (100%)
    pallas_call x1, Pallas kernels, shards(): pl.pallas_call(functools.partial(solve_kernel, n_seq, n_head), in_specs=[...  31.3 us
    pallas_call x1, Pallas kernels, shards(): pl.pallas_call(project_kernel, in_specs=[in_vmem, hbm, in_vmem], out_spec...  3.41 us

profile of v8, /device:TPU:7, one launch (start us, length us, event | category | flops | bytes accessed | tf_op | source)
XLA Modules:
  0.0 34.8 jit_solution(17116141333670819608)
XLA Ops:
  0.0 0.0 copy-start
  0.0 31.3 %solve.1 = (bf16[1024,512]{1,0:T(8,128)(2,1)S(1)}, bf16[3,2,4,64,512]{4,3,2,1,0:T(8,128)(2,1)S(1)}) custom-call(bf16[1024,512]{1,0:T(8,128)(2,1)} %k_hbm.1, bf16[1024,512]{1,0:T(8,128)(2,1)} %v_hbm.1, bf16[1024,512]{1,0:T(8,128)(2,1)} %q_hbm.1, f32[4,1024]{1,0:T(4,128)} %bitcast.1, f32[4]{0:T(128)} %ridge_ref.1, bf16[2048,512]{1,0:T(8,128)(2,1)} %w_hbm.3), custom_call_target="tpu_custom_call" | custom-call | flops 7784628224 | bytes 4194304 | tf_op jit(solution)/shard_map/solve/pallas_call | solution.py:432
  31.4 0.0 copy-done
  31.4 3.4 %project.1 = bf16[1,1024,2048]{2,1,0:T(8,128)(2,1)} custom-call(bf16[1024,512]{1,0:T(8,128)(2,1)S(1)} %get-tuple-element.7.readout, bf16[2048,512]{1,0:T(8,128)(2,1)S(1)} %copy-done, bf16[3,2,4,64,512]{4,3,2,1,0:T(8,128)(2,1)S(1)} %get-tuple-element.8.pieces_ref), custom_call_target="tpu_custom_call" | custom-call | flops 2147483648 | bytes 4194304 | tf_op jit(solution)/shard_map/project/pallas_call | solution.py:468
Async XLA Ops:
  0.0 31.4 %copy-start = (bf16[2048,512]{1,0:T(8,128)(2,1)S(1)}, bf16[2048,512]{1,0:T(8,128)(2,1)}, u32[]{:S(2)}) copy-start(bf16[2048,512]{1,0:T(8,128)(2,1)} %w_hbm.3) | copy-start | bytes 6291460

commit v9 on v8

--- a/solution.py
+++ b/solution.py
@@ -62,9 +62,13 @@
     GRAM, MOMENT = 0, 1
     chip_sums, slots = (chip_gram, chip_moment), (gram_slots, moment_slots)
 
+    near, far = pl.ds(0, half * HD), pl.ds(half * HD, half * HD)
     loads = [
         pltpu.make_async_copy(src, dst, load_sems.at[i])
-        for i, (src, dst) in enumerate(((k_hbm, k_ref), (v_hbm, v_ref), (q_hbm, q_ref)))
+        for i, (src, dst) in enumerate((
+            (k_hbm.at[:, near], k_ref.at[:, near]), (k_hbm.at[:, far], k_ref.at[:, far]),
+            (v_hbm, v_ref), (q_hbm, q_ref),
+        ))
     ]
     for load in loads:
         load.start()
@@ -108,7 +112,8 @@
             own[GRAM, h] = total
             return carry
 
-        lax.fori_loop(0, half, one, 0)
+        for j in range(half):
+            one(j, 0)
 
     def sum_moments(first):
         def one(j, carry):
@@ -125,7 +130,8 @@
             own[MOMENT, h] = total
             return carry
 
-        lax.fori_loop(0, half, one, 0)
+        for j in range(half):
+            one(j, 0)
 
     def heads_of(p):
         return pl.ds(p * half, half)
@@ -215,21 +221,23 @@
                 norms[n] = wide(square * scale * scale)
             return carry
 
-        lax.fori_loop(0, half, one, 0)
+        for j in range(half):
+            one(j, 0)
 
     loads[0].wait()
     sum_grams(0)
     pl.semaphore_wait(barrier, pairs + n_head - 1)
     to_mate(GRAM, 0).start()
+    loads[1].wait()
     sum_grams(half)
     pass_on(GRAM, 0)
     to_mate(GRAM, 1).start()
     for shift in range(1, n_head):
         to_head(shift).start()
-    loads[1].wait()
+    loads[2].wait()
     sum_moments(0)
     to_mate(MOMENT, 0).start()
-    loads[2].wait()
+    loads[3].wait()
     start_queries(0)
     collect(GRAM, 0)
     sum_moments(half)
@@ -276,7 +284,8 @@
                 sol[j * blocks + c] = jnp.zeros((SPAN, HD), f32)
             return carry
 
-        lax.fori_loop(0, half, prepare, 0)
+        for j in range(half):
+            prepare(j, 0)
 
         def multiply(n, fine=True):
             images[n] = apply(n, first * blocks + n, direct[n], gram_high, gram_low, keys_w, fine)
@@ -362,7 +371,8 @@
                 ).astype(out_ref.dtype)
             return carry
 
-        lax.fori_loop(0, half, finish, 0)
+        for j in range(half):
+            finish(j, 0)
         return carry
 
     lax.fori_loop(0, 2, run, 0)
@@ -448,7 +458,7 @@
             strip(2, 2, half), strip(2, half), strip(2, half, dtype=bf16),
             strip(2, pairs - 1, half), strip(2, pairs - 1, half, dtype=bf16),
             strip(2, 2, half), square(2, heads),
-            pltpu.SemaphoreType.DMA((3,)),
+            pltpu.SemaphoreType.DMA((4,)),
             pltpu.SemaphoreType.DMA((2, n_head - 1)),
             pltpu.SemaphoreType.DMA((2, 2)),
             pltpu.SemaphoreType.DMA((2, 2)),

time: 34.9 us -> 34.2 us (0.980)
  Pallas kernels: 34.8 us -> 34 us
    pallas_call x1, Pallas kernels: 31.3 us -> 30.6 us  [shards(): pl.pallas_call(functools.partial(solve_kernel, n_seq, n_head), in_specs=[...]
where the time goes in v9:
time: 34.2 us; the launch traced here: 34 us
  Pallas kernels  34 us (99%)
    pallas_call x1, Pallas kernels, shards(): pl.pallas_call(functools.partial(solve_kernel, n_seq, n_head), in_specs=[...  30.6 us
    pallas_call x1, Pallas kernels, shards(): pl.pallas_call(project_kernel, in_specs=[in_vmem, hbm, in_vmem], out_spec...  3.41 us

profile of v9, /device:TPU:7, one launch (start us, length us, event | category | flops | bytes accessed | tf_op | source)
XLA Modules:
  0.0 34.0 jit_solution(14941382756366928452)
XLA Ops:
  0.0 0.0 copy-start
  0.0 30.6 %solve.1 = (bf16[1024,512]{1,0:T(8,128)(2,1)S(1)}, bf16[3,2,4,64,512]{4,3,2,1,0:T(8,128)(2,1)S(1)}) custom-call(bf16[1024,512]{1,0:T(8,128)(2,1)} %k_hbm.1, bf16[1024,512]{1,0:T(8,128)(2,1)} %v_hbm.1, bf16[1024,512]{1,0:T(8,128)(2,1)} %q_hbm.1, f32[4,1024]{1,0:T(4,128)} %bitcast.1, f32[4]{0:T(128)} %ridge_ref.1, bf16[2048,512]{1,0:T(8,128)(2,1)} %w_hbm.3), custom_call_target="tpu_custom_call" | custom-call | flops 7784628224 | bytes 4194304 | tf_op jit(solution)/shard_map/solve/pallas_call | solution.py:442
  30.6 0.0 copy-done
  30.6 3.4 %project.1 = bf16[1,1024,2048]{2,1,0:T(8,128)(2,1)} custom-call(bf16[1024,512]{1,0:T(8,128)(2,1)S(1)} %get-tuple-element.7.readout, bf16[2048,512]{1,0:T(8,128)(2,1)S(1)} %copy-done, bf16[3,2,4,64,512]{4,3,2,1,0:T(8,128)(2,1)S(1)} %get-tuple-element.8.pieces_ref), custom_call_target="tpu_custom_call" | custom-call | flops 2147483648 | bytes 4194304 | tf_op jit(solution)/shard_map/project/pallas_call | solution.py:478
Async XLA Ops:
  0.0 30.6 %copy-start = (bf16[2048,512]{1,0:T(8,128)(2,1)S(1)}, bf16[2048,512]{1,0:T(8,128)(2,1)}, u32[]{:S(2)}) copy-start(bf16[2048,512]{1,0:T(8,128)(2,1)} %w_hbm.3) | copy-start | bytes 6291460

commit v10 on v9

--- a/solution.py
+++ b/solution.py
@@ -70,8 +70,7 @@
             (v_hbm, v_ref), (q_hbm, q_ref),
         ))
     ]
-    for load in loads:
-        load.start()
+    loads[0].start()
 
     barrier = pltpu.get_barrier_semaphore()
     pl.semaphore_signal(barrier, inc=1, device_id=mate_at, device_id_type=MESH)
@@ -225,6 +224,8 @@
             one(j, 0)
 
     loads[0].wait()
+    for load in loads[1:]:
+        load.start()
     sum_grams(0)
     pl.semaphore_wait(barrier, pairs + n_head - 1)
     to_mate(GRAM, 0).start()

time: 34.2 us -> 34.2 us (level)
  no operation moved by 1% of the time
where the time goes in v10:
time: 34.2 us; the launch traced here: 34 us
  Pallas kernels  34 us (99%)
    pallas_call x1, Pallas kernels, shards(): pl.pallas_call(functools.partial(solve_kernel, n_seq, n_head), in_specs=[...  30.6 us
    pallas_call x1, Pallas kernels, shards(): pl.pallas_call(project_kernel, in_specs=[in_vmem, hbm, in_vmem], out_spec...  3.41 us

profile of v10, /device:TPU:7, one launch (start us, length us, event | category | flops | bytes accessed | tf_op | source)
XLA Modules:
  0.0 34.0 jit_solution(10038236915651298557)
XLA Ops:
  0.0 0.0 copy-start
  0.0 30.6 %solve.1 = (bf16[1024,512]{1,0:T(8,128)(2,1)S(1)}, bf16[3,2,4,64,512]{4,3,2,1,0:T(8,128)(2,1)S(1)}) custom-call(bf16[1024,512]{1,0:T(8,128)(2,1)} %k_hbm.1, bf16[1024,512]{1,0:T(8,128)(2,1)} %v_hbm.1, bf16[1024,512]{1,0:T(8,128)(2,1)} %q_hbm.1, f32[4,1024]{1,0:T(4,128)} %bitcast.1, f32[4]{0:T(128)} %ridge_ref.1, bf16[2048,512]{1,0:T(8,128)(2,1)} %w_hbm.3), custom_call_target="tpu_custom_call" | custom-call | flops 7784628224 | bytes 4194304 | tf_op jit(solution)/shard_map/solve/pallas_call | solution.py:443
  30.6 0.0 copy-done
  30.6 3.4 %project.1 = bf16[1,1024,2048]{2,1,0:T(8,128)(2,1)} custom-call(bf16[1024,512]{1,0:T(8,128)(2,1)S(1)} %get-tuple-element.7.readout, bf16[2048,512]{1,0:T(8,128)(2,1)S(1)} %copy-done, bf16[3,2,4,64,512]{4,3,2,1,0:T(8,128)(2,1)S(1)} %get-tuple-element.8.pieces_ref), custom_call_target="tpu_custom_call" | custom-call | flops 2147483648 | bytes 4194304 | tf_op jit(solution)/shard_map/project/pallas_call | solution.py:479
Async XLA Ops:
  0.0 30.6 %copy-start = (bf16[2048,512]{1,0:T(8,128)(2,1)S(1)}, bf16[2048,512]{1,0:T(8,128)(2,1)}, u32[]{:S(2)}) copy-start(bf16[2048,512]{1,0:T(8,128)(2,1)} %w_hbm.3) | copy-start | bytes 6291460
